TPU v7x, 8 devices: a whole 2x2x1 slice. The times are simulated.
8 devices in a mesh: ty: 2 (over z, y), tx: 4 (over x, core).
Axes of the slice: x: 2, y: 2, z: 1, core: 2. Of those that a mesh axis runs over, the one named last changes fastest.
Arguments:
- x_tok: bfloat16 [4096, 512], P('ty', 'tx')
- dy_tok: bfloat16 [4096, 512], P('ty', 'tx')
- ln_gain: float32 [512], P('tx')
- w_gate: bfloat16 [512, 2048], P('tx', 'ty')
- w_up: bfloat16 [512, 2048], P('tx', 'ty')
- w_down: bfloat16 [2048, 512], P('ty', 'tx')
Outputs:
- output 1: bfloat16 [4096, 512], P('ty', 'tx')
- output 2: bfloat16 [4096, 512], P('ty', 'tx')
- output 3: float32 [512, 2048], P('tx', 'ty')
- output 4: float32 [512, 2048], P('tx', 'ty')
- output 5: float32 [2048, 512], P('ty', 'tx')
- output 6: float32 [512], P('tx')
All inputs are finite; a program needn't handle non-finite values.
Results may differ from a plain program's by a relative error of at most 0.001.
Values are sent between devices in bfloat16 or wider.
A program may use at most 1 GiB of HBM per device.

v0:
```python
import jax
import jax.numpy as jnp
from jax import lax
from jax.sharding import PartitionSpec as P

LN_EPS = 1e-6


def contract_rows(left_op, right_op):
    return lax.dot_general(left_op, right_op, (((0,), (0,)), ((), ())), preferred_element_type=jnp.float32)


def contract_cols(left_op, right_op):
    return lax.dot_general(left_op, right_op, (((1,), (1,)), ((), ())), preferred_element_type=jnp.float32)


def solution(mesh):
    tx_size = mesh.shape["tx"]

    def local_step(x_blk, dy_blk, gain_blk, w_gate_blk, w_up_blk, w_down_blk):
        d_model = x_blk.shape[1] * tx_size
        x_float = x_blk.astype(jnp.float32)
        ln_stats = lax.psum(jnp.stack([jnp.sum(x_float, axis=1), jnp.sum(x_float * x_float, axis=1)]), "tx") / d_model
        mean_x = ln_stats[0][:, None]
        inv_std = lax.rsqrt(ln_stats[1][:, None] - mean_x * mean_x + LN_EPS)
        x_hat = (x_float - mean_x) * inv_std
        h_blk = (gain_blk * x_hat).astype(jnp.bfloat16)
        h_all = lax.all_gather(h_blk, "ty", axis=0, tiled=True)
        gate_pre = lax.psum_scatter(jnp.dot(h_all, w_gate_blk, preferred_element_type=jnp.float32),
                                    "tx", scatter_dimension=0, tiled=True)
        up_pre = lax.psum_scatter(jnp.dot(h_all, w_up_blk, preferred_element_type=jnp.float32),
                                  "tx", scatter_dimension=0, tiled=True)
        gate_sig = jax.nn.sigmoid(gate_pre)
        gate_swish = gate_pre * gate_sig
        act_blk = (gate_swish * up_pre).astype(jnp.bfloat16)
        act_all = lax.all_gather(act_blk, "tx", axis=0, tiled=True)
        mlp_out = lax.psum_scatter(jnp.dot(act_all, w_down_blk, preferred_element_type=jnp.float32),
                                   "ty", scatter_dimension=0, tiled=True)
        y_blk = (x_float + mlp_out).astype(jnp.bfloat16)

        dy_all = lax.all_gather(dy_blk, "ty", axis=0, tiled=True)
        dw_down_blk = contract_rows(act_all, dy_all)
        d_act = lax.psum_scatter(contract_cols(dy_all, w_down_blk), "tx", scatter_dimension=0, tiled=True)
        d_gate = (d_act * up_pre * gate_sig * (1.0 + gate_pre * (1.0 - gate_sig))).astype(jnp.bfloat16)
        d_up = (d_act * gate_swish).astype(jnp.bfloat16)
        d_gate_all = lax.all_gather(d_gate, "tx", axis=0, tiled=True)
        d_up_all = lax.all_gather(d_up, "tx", axis=0, tiled=True)
        dw_gate_blk = contract_rows(h_all, d_gate_all)
        dw_up_blk = contract_rows(h_all, d_up_all)
        d_hnorm = lax.psum_scatter(contract_cols(d_gate_all, w_gate_blk) + contract_cols(d_up_all, w_up_blk),
                                   "ty", scatter_dimension=0, tiled=True)
        value_a6 = d_hnorm * gain_blk
        bwd_stats = lax.psum(jnp.stack([jnp.sum(value_a6, axis=1), jnp.sum(value_a6 * x_hat, axis=1)]), "tx") / d_model
        dx_ln = inv_std * (value_a6 - bwd_stats[0][:, None] - x_hat * bwd_stats[1][:, None])
        dx_blk = (dy_blk.astype(jnp.float32) + dx_ln).astype(jnp.bfloat16)
        d_gain_blk = lax.psum(jnp.sum(d_hnorm * x_hat, axis=0), "ty")
        return (y_blk, dx_blk, dw_gate_blk, dw_up_blk, dw_down_blk, d_gain_blk)

    return jax.shard_map(
        local_step, mesh=mesh,
        in_specs=(P("ty", "tx"), P("ty", "tx"), P("tx"), P("tx", "ty"), P("tx", "ty"), P("ty", "tx")),
        out_specs=(P("ty", "tx"), P("ty", "tx"), P("tx", "ty"), P("tx", "ty"), P("ty", "tx"), P("tx")),
        check_vma=False)
```

profile of v0, /device:TPU:0, one launch (start us, length us, event | category | flops | bytes accessed | tf_op | source)
XLA Modules:
  0.0 678.6 jit_solution(6900350262868304880)
XLA Ops:
  7.2 1.6 convert_reduce_fusion
  8.8 13.1 %psum.21 = f32[2,2048]{1,0:T(2,128)S(1)} all-reduce(f32[2,2048]{1,0:T(2,128)S(1)} %pad_maximum_fusion), channel_id=1, replica_groups=mesh['ty'=2,'tx'=4] {'tx'}, use_global_device_ids=true, to_apply=%region_2.0 | all-reduce | flops 4096 | bytes 32768 | tf_op jit(solution)/shard_map/psum | solution.py:23
  21.9 2.4 fusion.7
  24.4 0.7 all-gather.10.cloned.1.call-update
  25.2 17.7 %all-gather.6.cloned.1.call-done = bf16[4096,128]{1,0:T(8,128)(2,1)} async-done(((bf16[2048,128]{1,0:T(8,128)(2,1)}), bf16[4096,128]{1,0:T(8,128)(2,1)}) %all-gather.6.cloned.1.call-update) | async-done | bytes 1048592 | tf_op jit(solution)/shard_map/all_gather | solution.py:28
  42.9 9.3 %fusion.18 = f32[4096,1024]{1,0:T(8,128)} fusion(bf16[4096,128]{1,0:T(8,128)(2,1)} %all-gather.6.cloned.1.call-done, bf16[128,1024]{1,0:T(8,128)(2,1)} %param.10), kind=kOutput, calls=%fused_computation.33 | convolution fusion | flops 1073741824 | bytes 18087936 | tf_op jit(solution)/shard_map/dot_general | solution.py:31
  52.3 1.1 copy-done.1
  53.4 8.1 %fusion.17 = f32[4096,1024]{1,0:T(8,128)} fusion(bf16[4096,128]{1,0:T(8,128)(2,1)S(1)} %copy-done.1, bf16[128,1024]{1,0:T(8,128)(2,1)S(1)} %copy-done), kind=kOutput, calls=%fused_computation.32 | convolution fusion | flops 1073741824 | bytes 18087936 | tf_op jit(solution)/shard_map/dot_general | solution.py:29
  61.6 1.1 all-gather.10.cloned.1.call-done
  62.7 9.3 %fusion.20 = f32[4096,1024]{1,0:T(8,128)} fusion(bf16[4096,128]{1,0:T(8,128)(2,1)} %all-gather.10.cloned.1.call-done, bf16[1024,128]{1,0:T(8,128)(2,1)S(1)} %copy-done.5), kind=kOutput, calls=%fused_computation.35 | convolution fusion | flops 1073741824 | bytes 18087936 | tf_op jit(solution)/shard_map/dot_general | solution.py:14
  72.0 112.0 %reduce-scatter.8.cloned.1.call-done = f32[1024,1024]{1,0:T(8,128)} async-done(((f32[4096,1024]{1,0:T(8,128)}), f32[1024,1024]{1,0:T(8,128)}) %reduce-scatter.8.cloned.1.call-update) | async-done | bytes 4194320 | tf_op jit(solution)/shard_map/reduce_scatter | solution.py:31
  184.0 121.2 %reduce-scatter.6.cloned.1.call-done = f32[1024,1024]{1,0:T(8,128)} async-done(((f32[4096,1024]{1,0:T(8,128)}), f32[1024,1024]{1,0:T(8,128)}) %reduce-scatter.6.cloned.1.call-update) | async-done | bytes 4194320 | tf_op jit(solution)/shard_map/reduce_scatter | solution.py:29
  305.2 121.2 %reduce-scatter.12.cloned.1.call-done = f32[1024,1024]{1,0:T(8,128)} async-done(((f32[4096,1024]{1,0:T(8,128)}), f32[1024,1024]{1,0:T(8,128)}) %reduce-scatter.12.cloned.1.call-update) | async-done | bytes 4194320 | tf_op jit(solution)/shard_map/reduce_scatter | solution.py:43
  426.3 8.4 %multiply_convert_fusion = (bf16[1024,1024]{1,0:T(8,128)(2,1)}, bf16[1024,1024]{1,0:T(8,128)(2,1)}, bf16[1024,1024]{1,0:T(8,128)(2,1)}) fusion(f32[1024,1024]{1,0:T(8,128)} %reduce-scatter.12.cloned.1.call-done, f32[1024,1024]{1,0:T(8,128)} %reduce-scatter.6.cloned.1.call-done, f32[1024,1024]{1,0:T(8,128)} %reduce-scatter.8.cloned.1.call-done), kind=kLoop, calls=%fused_computation.1 | loop fusion | flops 15728640 | bytes 18874368 | tf_op jit(solution)/shard_map/convert_element_type | solution.py:45
  434.8 0.7 all-gather.14.cloned.1.call-update
  435.6 0.7 all-gather.8.cloned.1.call-update
  436.3 0.2 reduce-scatter.14.cloned.1.call-start
  436.5 54.2 %all-gather.12.cloned.1.call-done = bf16[4096,1024]{1,0:T(8,128)(2,1)} async-done(((bf16[1024,1024]{1,0:T(8,128)(2,1)}), bf16[4096,1024]{1,0:T(8,128)(2,1)}) %all-gather.12.cloned.1.call-update) | async-done | bytes 8388624 | tf_op jit(solution)/shard_map/all_gather | solution.py:46
  490.7 5.7 fusion.21
  496.4 51.5 %all-gather.14.cloned.1.call-done = bf16[4096,1024]{1,0:T(8,128)(2,1)} async-done(((bf16[1024,1024]{1,0:T(8,128)(2,1)}), bf16[4096,1024]{1,0:T(8,128)(2,1)}) %all-gather.14.cloned.1.call-update) | async-done | bytes 8388624 | tf_op jit(solution)/shard_map/all_gather | solution.py:47
  547.9 7.1 %convolution_add_fusion = f32[4096,128]{1,0:T(8,128)} fusion(f32[4096,128]{1,0:T(8,128)S(1)} %fusion.21, bf16[4096,1024]{1,0:T(8,128)(2,1)} %all-gather.14.cloned.1.call-done, bf16[128,1024]{1,0:T(8,128)(2,1)} %param.10), kind=kOutput, calls=%fused_computation | convolution fusion | flops 1074266112 | bytes 12845056 | tf_op jit(solution)/shard_map/dot_general | solution.py:14
  555.1 50.1 %all-gather.8.cloned.1.call-done = bf16[4096,1024]{1,0:T(8,128)(2,1)} async-done(((bf16[1024,1024]{1,0:T(8,128)(2,1)}), bf16[4096,1024]{1,0:T(8,128)(2,1)}) %all-gather.8.cloned.1.call-update) | async-done | bytes 8388624 | tf_op jit(solution)/shard_map/all_gather | solution.py:36
  605.2 7.1 %fusion.19 = f32[4096,128]{1,0:T(8,128)} fusion(bf16[4096,1024]{1,0:T(8,128)(2,1)} %all-gather.8.cloned.1.call-done, bf16[1024,128]{1,0:T(8,128)(2,1)} %param.11), kind=kOutput, calls=%fused_computation.34 | convolution fusion | flops 1073741824 | bytes 10747904 | tf_op jit(solution)/shard_map/dot_general | solution.py:37
  612.4 5.6 fusion.22
  618.0 5.6 fusion.23
  623.6 3.1 fusion.24
  626.8 9.7 %reduce-scatter.14.cloned.1.call-done = f32[2048,128]{1,0:T(8,128)} async-done(((f32[4096,128]{1,0:T(8,128)}), f32[2048,128]{1,0:T(8,128)}) %reduce-scatter.14.cloned.1.call-update) | async-done | bytes 1048592 | tf_op jit(solution)/shard_map/reduce_scatter | solution.py:50
  636.5 2.3 fusion.13
  638.8 5.5 psum.23
  644.3 10.9 %psum.22 = f32[2,2048]{1,0:T(2,128)S(1)} all-reduce(f32[2,2048]{1,0:T(2,128)S(1)} %pad_maximum_fusion.1), channel_id=1, replica_groups=mesh['ty'=2,'tx'=4] {'tx'}, use_global_device_ids=true, to_apply=%region_10.0 | all-reduce | flops 4096 | bytes 32768 | tf_op jit(solution)/shard_map/psum | solution.py:53
  655.3 12.4 %reduce-scatter.10.cloned.1.call-done = f32[2048,128]{1,0:T(8,128)} async-done(((f32[4096,128]{1,0:T(8,128)}), f32[2048,128]{1,0:T(8,128)}) %reduce-scatter.10.cloned.1.call-update) | async-done | bytes 1048592 | tf_op jit(solution)/shard_map/reduce_scatter | solution.py:37
  667.6 4.1 fusion.12
  (41 shorter events, 0.6 us)
Async XLA Ops:
  7.2 45.1 %copy-start = (bf16[128,1024]{1,0:T(8,128)(2,1)S(1)}, bf16[128,1024]{1,0:T(8,128)(2,1)}, u32[]{:S(2)}) copy-start(bf16[128,1024]{1,0:T(8,128)(2,1)} %param.9) | copy-start | bytes 786436
  7.2 35.7 %all-gather.6.cloned.1.call-start = ((), (), s32[]{:S(2)}) async-start(), calls=%async_computation.5 | async-start | bytes 1572864 | tf_op jit(solution)/shard_map/all_gather | solution.py:28
  24.4 38.3 %all-gather.10.cloned.1.call-start = ((), (), s32[]{:S(2)}) async-start(), calls=%async_computation.10 | async-start | bytes 1572864 | tf_op jit(solution)/shard_map/all_gather | solution.py:41
  25.1 158.8 %reduce-scatter.8.cloned.1.call-start = ((), (), s32[]{:S(2)}) async-start(), calls=%async_computation.7 | async-start | bytes 20971520 | tf_op jit(solution)/shard_map/reduce_scatter | solution.py:31
  52.2 1.2 copy-start.1
  52.2 252.9 %reduce-scatter.6.cloned.1.call-start = ((), (), s32[]{:S(2)}) async-start(), calls=%async_computation.6 | async-start | bytes 20971520 | tf_op jit(solution)/shard_map/reduce_scatter | solution.py:29
  61.5 1.2 copy-start.5
  61.5 364.8 %reduce-scatter.12.cloned.1.call-start = ((), (), s32[]{:S(2)}) async-start(), calls=%async_computation.11 | async-start | bytes 20971520 | tf_op jit(solution)/shard_map/reduce_scatter | solution.py:43
  72.0 418.7 %all-gather.12.cloned.1.call-start = ((), (), s32[]{:S(2)}) async-start(), calls=%async_computation.12 | async-start | bytes 10485760 | tf_op jit(solution)/shard_map/all_gather | solution.py:46
  434.8 113.2 %all-gather.14.cloned.1.call-start = ((), (), s32[]{:S(2)}) async-start(), calls=%async_computation.13 | async-start | bytes 10485760 | tf_op jit(solution)/shard_map/all_gather | solution.py:47
  435.5 169.7 %all-gather.8.cloned.1.call-start = ((), (), s32[]{:S(2)}) async-start(), calls=%async_computation.8 | async-start | bytes 10485760 | tf_op jit(solution)/shard_map/all_gather | solution.py:36
  436.3 200.2 %reduce-scatter.14.cloned.1.call-start = ((), (), s32[]{:S(2)}) async-start(), calls=%async_computation.14 | async-start | bytes 3145728 | tf_op jit(solution)/shard_map/reduce_scatter | solution.py:50
  555.0 112.6 %reduce-scatter.10.cloned.1.call-start = ((), (), s32[]{:S(2)}) async-start(), calls=%async_computation.9 | async-start | bytes 3145728 | tf_op jit(solution)/shard_map/reduce_scatter | solution.py:37
  612.4 11.2 %slice-start = ((s8[8388608]{0:T(1024)(128)(4,1)}), s8[4194304]{0:T(1024)(128)(4,1)S(1)}, s32[]{:S(2)}) async-start(s8[8388608]{0:T(1024)(128)(4,1)} %bitcast.26), calls=%async_computation.15 | async-start | bytes 8388608
  618.0 5.6 slice-start.1
  618.0 5.6 copy-start.4
  623.6 12.9 %copy-start.2 = (bf16[2048,128]{1,0:T(8,128)(2,1)S(1)}, bf16[2048,128]{1,0:T(8,128)(2,1)}, u32[]{:S(2)}) copy-start(bf16[2048,128]{1,0:T(8,128)(2,1)} %param.6) | copy-start | bytes 1572868
  623.6 12.9 %copy-start.6 = (f32[128]{0:T(128)S(1)}, f32[128]{0:T(128)}, u32[]{:S(2)}) copy-start(f32[128]{0:T(128)} %param.8) | copy-start | bytes 1540
  623.6 44.0 %copy-start.3 = (bf16[2048,128]{1,0:T(8,128)(2,1)S(1)}, bf16[2048,128]{1,0:T(8,128)(2,1)}, u32[]{:S(2)}) copy-start(bf16[2048,128]{1,0:T(8,128)(2,1)} %param.7) | copy-start | bytes 1572868
Sparse Core Ops, SparseCore 0:
  24.5 18.2 all-gather.5
  44.4 18.2 all-gather.9
  65.2 118.7 reduce-scatter.7
  186.4 118.7 reduce-scatter.5
  307.5 118.7 reduce-scatter.11
  434.9 55.7 all-gather.11
  492.2 55.7 all-gather.13
  549.5 55.7 all-gather.7
  607.4 29.0 reduce-scatter.13
  638.6 29.0 reduce-scatter.9
where the time goes:
time: 679 us
  waiting for transfers between devices  553 us (81%)
  matrix products  60.9 us (9%)
  blocking collectives  29.4 us (4%)
  other arithmetic  19 us (3%)
  between operations  14.3 us (2%)
    reduce_scatter x1, waiting for transfers between devices, local_step(): lax.psum_scatter(jnp.dot(h_all, w_gate_blk, preferred_element_type=jnp.fl...  121 us
    reduce_scatter x1, waiting for transfers between devices, local_step(): lax.psum_scatter(contract_cols(dy_all, w_down_blk), 'tx', scatter_dimensi...  121 us
    reduce_scatter x1, waiting for transfers between devices, local_step(): lax.psum_scatter(jnp.dot(h_all, w_up_blk, preferred_element_type=jnp.floa...  112 us
    all_gather x1, waiting for transfers between devices, local_step(): d_gate_all = lax.all_gather(d_gate, 'tx', axis=0, tiled=True)  54.2 us
    all_gather x1, waiting for transfers between devices, local_step(): d_up_all = lax.all_gather(d_up, 'tx', axis=0, tiled=True)  51.5 us
    all_gather x1, waiting for transfers between devices, local_step(): act_all = lax.all_gather(act_blk, 'tx', axis=0, tiled=True)  50.1 us
    dot_general x3, matrix products, contract_cols(): lax.dot_general(left_op, right_op, (((1,), (1,)), ((), ())), preferred_el...  22.1 us
    all_gather x1, waiting for transfers between devices, local_step(): h_all = lax.all_gather(h_blk, 'ty', axis=0, tiled=True)  17.7 us
  transfers between devices with their start and end apart: 10, of which 10 were waited for; matrix products, arithmetic and copies ran while one was open for 9% of the time, Pallas kernels for 0%

commit v1 on v0

v1 whole, which is shorter than its diff:
```python
import jax
import jax.numpy as jnp
from jax import lax
from jax.experimental import pallas as pl
from jax.experimental.pallas import tpu as pltpu
from jax.sharding import PartitionSpec as P

LN_EPS = 1e-6
MESH = pl.DeviceIdType.MESH
F32 = jnp.float32
BF16 = jnp.bfloat16

OWN, PAIR, NEAR, DIAG = 0, 1, 2, 3
CHUNKS = 4
LN_ROWS = 128
ROW_TILE = 256


def dot(a, b):
    return lax.dot_general(a, b, (((1,), (0,)), ((), ())), preferred_element_type=F32)


def dot_nt(a, b):
    return lax.dot_general(a, b, (((1,), (1,)), ((), ())), preferred_element_type=F32)


def kernel(x_in, dy_in, g_in, w1_in, w3_in, w2_in,
           y_out, dx_out, dw1_out, dw3_out, dw2_out, dg_out,
           xg, dyg, gg, w1g, w3g, w2g, h, h_t, dy_t, act, du, dv, part, pair_in, summed, link_in,
           m_acc, dh_acc, y_st, dx_st, dw_st, dw2_st, dg_st, dg_in,
           g_send, g_recv, in_send, in_recv, fw_send, fw_recv, w_send, w_recv, dw_send, dw_recv,
           lk_send, lk_recv, out_send, out_recv, dg_send, dg_recv, lc_in, lc_w, lc_g, lc_out, lc_dw):
    y, t = lax.axis_index("ty"), lax.axis_index("tx")
    x, c = t // 2, t % 2
    tok = x_in.shape[0] // 4
    wid = x_in.shape[1]
    fc = w1_in.shape[1] // CHUNKS
    d = 4 * wid
    peer_t = (t, 2 * x + 1 - c, 2 * (1 - x) + c, 2 * (1 - x) + 1 - c)
    dev = {r: (y, peer_t[r]) for r in (PAIR, NEAR, DIAG)}
    cross = (1 - y, t)

    barrier = pltpu.get_barrier_semaphore()
    for ya in (y, 1 - y):
        for r in range(4):
            if ya is y and r == OWN:
                continue
            pl.semaphore_signal(barrier, inc=1, device_id=(ya, peer_t[r]), device_id_type=MESH)
    pl.semaphore_wait(barrier, 7)

    def remote(src, dst, send, recv, to):
        return pltpu.make_async_remote_copy(src_ref=src, dst_ref=dst, send_sem=send, recv_sem=recv,
                                            device_id=to, device_id_type=MESH)

    def col(r):
        return pl.ds(pl.multiple_of(peer_t[r] * wid, wid), wid)

    def rows_of(r):
        return pl.ds(pl.multiple_of(peer_t[r] * tok, tok), tok)

    mine, other = pl.ds(0, tok), pl.ds(tok, tok)
    tin, tg = (x_in, dy_in), (xg, dyg)

    def in_copy(i, r):
        return remote(tin[i].at[rows_of(r), :], tg[i].at[mine, col(OWN)], in_send.at[i, r], in_recv.at[i, r], dev[r])

    def fw_copy(i, r):
        src = tin[i].at[rows_of(OWN), :] if r == OWN else tg[i].at[mine, col(r)]
        return remote(src, tg[i].at[other, col(r)], fw_send.at[i, r], fw_recv.at[i, r], cross)

    def own_copy(i):
        return pltpu.make_async_copy(tin[i].at[rows_of(OWN), :], tg[i].at[mine, col(OWN)], lc_in.at[i])

    def g_copy(r):
        return remote(g_in, gg.at[t], g_send.at[r], g_recv.at[r], dev[r])

    def w_src(w, j):
        if w == 2:
            return w2_in.at[pl.ds(j * fc, fc), :]
        return (w1_in, w3_in)[w].at[:, pl.ds(j * fc, fc)]

    def w_dst(w, j, r):
        if w == 2:
            return w2g.at[j, :, col(r)]
        return (w1g, w3g)[w].at[j, col(r), :]

    def w_copy(kind, w, j):
        if kind == 0:
            src, dst, to = w_src(w, j), w_dst(w, j, OWN), dev[NEAR]
        elif kind == 1:
            src, dst, to = w_src(w, j), w_dst(w, j, OWN), dev[PAIR]
        elif kind == 2:
            src, dst, to = w_dst(w, j, NEAR), w_dst(w, j, NEAR), dev[PAIR]
        elif kind == 3:
            src, dst, to = w_src(w, j), w_dst(w, CHUNKS + j, OWN), cross
        elif kind == 4:
            src, dst, to = w_dst(w, j, NEAR), w_dst(w, CHUNKS + j, NEAR), cross
        elif kind == 5:
            src, dst, to = w_dst(w, CHUNKS + j, OWN), w_dst(w, CHUNKS + j, OWN), dev[PAIR]
        else:
            src, dst, to = w_dst(w, CHUNKS + j, NEAR), w_dst(w, CHUNKS + j, NEAR), dev[PAIR]
        return remote(src, dst, w_send.at[kind, w, j], w_recv.at[kind, w, j], to)

    def own_w(w, j):
        return pltpu.make_async_copy(w_src(w, j), w_dst(w, j, OWN), lc_w.at[w, j])

    for r in (NEAR, DIAG):
        in_copy(0, r).start()
    for i in range(2):
        in_copy(i, PAIR).start()
        fw_copy(i, OWN).start()
    for r in (PAIR, NEAR, DIAG):
        g_copy(r).start()
    own_g = pltpu.make_async_copy(g_in, gg.at[t], lc_g)
    own_g.start()
    for i in range(2):
        own_copy(i).start()
    for r in (NEAR, DIAG):
        in_copy(1, r).start()
    for j in range(CHUNKS):
        for w in range(3):
            w_copy(0, w, j).start()
            w_copy(1, w, j).start()
            own_w(w, j).start()

    for i in range(2):
        in_copy(i, PAIR).wait_recv()
        fw_copy(i, PAIR).start()
    for r in (NEAR, DIAG):
        in_copy(0, r).wait_recv()
        fw_copy(0, r).start()
    own_copy(0).wait()
    own_g.wait()
    for r in (PAIR, NEAR, DIAG):
        g_copy(r).wait_recv()
    gain = jnp.concatenate([gg[k] for k in range(4)], axis=1)

    def norm(rows):
        xf = xg[rows, :].astype(F32)
        mu = jnp.sum(xf, axis=1, keepdims=True) * (1.0 / d)
        s = jnp.sum(xf * xf, axis=1, keepdims=True) * (1.0 / d)
        inv = lax.rsqrt(s - mu * mu + LN_EPS)
        return xf, (xf - mu) * inv, inv

    def ln_rows(base):
        def body(k, carry):
            rows = pl.ds(pl.multiple_of(base + k * LN_ROWS, LN_ROWS), LN_ROWS)
            _, xhat, _ = norm(rows)
            hb = (gain * xhat).astype(BF16)
            h[rows, :] = hb
            h_t[:, rows] = hb.astype(F32).T.astype(BF16)
            return carry
        lax.fori_loop(0, tok // LN_ROWS, body, 0)

    def dy_rows(base):
        def body(k, carry):
            rows = pl.ds(pl.multiple_of(base + k * LN_ROWS, LN_ROWS), LN_ROWS)
            dy_t[:, rows] = dyg[rows, :].astype(F32).T.astype(BF16)
            return carry
        lax.fori_loop(0, tok // LN_ROWS, body, 0)

    ln_rows(0)
    for r in (NEAR, DIAG):
        in_copy(1, r).wait_recv()
        fw_copy(1, r).start()
    own_copy(1).wait()
    dy_rows(0)

    def pass_w(j):
        for w in range(3):
            w_copy(3, w, j).start()
        for w in range(3):
            w_copy(0, w, j).wait_recv()
            w_copy(2, w, j).start()
            w_copy(4, w, j).start()

    pass_w(0)
    for r in range(4):
        fw_copy(0, r).wait_recv()
    ln_rows(tok)
    pass_w(1)
    for r in range(4):
        fw_copy(1, r).wait_recv()
    dy_rows(tok)

    m_acc[...] = jnp.zeros_like(m_acc)
    dh_acc[...] = jnp.zeros_like(dh_acc)

    def gated(j, n):
        def body(k, carry):
            rows = pl.ds(pl.multiple_of(k * ROW_TILE, ROW_TILE), ROW_TILE)
            hr = h[rows, :]
            u = dot(hr, w1g[j])
            v = dot(hr, w3g[j])
            da = dot_nt(dyg[rows, :], w2g[j])
            sig = 1.0 / (1.0 + jnp.exp(-u))
            swish = u * sig
            act[rows, :] = (swish * v).astype(BF16)
            du[rows, :] = (da * v * sig * (1.0 + u * (1.0 - sig))).astype(BF16)
            dv[rows, :] = (da * swish).astype(BF16)
            return carry
        lax.fori_loop(0, n // ROW_TILE, body, 0)

    def to_tokens(j):
        def body(k, carry):
            rows = pl.ds(pl.multiple_of(k * ROW_TILE, ROW_TILE), ROW_TILE)
            m_acc[rows, :] += dot(act[rows, :], w2g[j])
            dh_acc[rows, :] += dot_nt(du[rows, :], w1g[j]) + dot_nt(dv[rows, :], w3g[j])
            return carry
        lax.fori_loop(0, tok // ROW_TILE, body, 0)

    def pair_copy(far, j):
        block = peer_t[DIAG] if far else peer_t[PAIR]
        return remote(part.at[j, block], pair_in.at[far, j], dw_send.at[far, j], dw_recv.at[far, j], dev[PAIR])

    def link_copy(j):
        return remote(summed.at[j], link_in.at[j], lk_send.at[j], lk_recv.at[j], dev[NEAR])

    for j in range(CHUNKS):
        for w in range(3):
            own_w(w, j).wait()
            w_copy(1, w, j).wait_recv()
            w_copy(2, w, j).wait_recv()
        gated(j, 2 * tok)
        for k, (left, right) in enumerate(((h_t, du), (h_t, dv), (dy_t, act))):
            full = dot(left[...], right[...])
            for b in range(4):
                part[j, b, k * wid:(k + 1) * wid, :] = full[b * wid:(b + 1) * wid, :]
        pair_copy(1, j).start()
        pair_copy(0, j).start()
        to_tokens(j)
        pair_copy(1, j).wait_recv()
        summed[j] = part[j, peer_t[NEAR]] + pair_in[1, j]
        link_copy(j).start()
        if j + 2 < CHUNKS:
            pass_w(j + 2)

    def dw_outs(j):
        cols = pl.ds(j * fc, fc)
        return (pltpu.make_async_copy(dw_st.at[j, 0], dw1_out.at[:, cols], lc_dw.at[0, j]),
                pltpu.make_async_copy(dw_st.at[j, 1], dw3_out.at[:, cols], lc_dw.at[1, j]),
                pltpu.make_async_copy(dw2_st.at[j], dw2_out.at[cols, :], lc_dw.at[2, j]))

    def finish_dw(j):
        pair_copy(0, j).wait_recv()
        link_copy(j).wait_recv()
        total = part[j, t] + pair_in[0, j] + link_in[j]
        dw_st[j, 0] = total[:wid, :]
        dw_st[j, 1] = total[wid:2 * wid, :]
        dw2_st[j] = total[2 * wid:, :].T
        for cp in dw_outs(j):
            cp.start()

    for j in range(CHUNKS):
        for w in range(3):
            w_copy(3, w, j).wait_recv()
            w_copy(5, w, j).start()
        for w in range(3):
            w_copy(4, w, j).wait_recv()
            w_copy(6, w, j).start()
        for w in range(3):
            w_copy(5, w, j).wait_recv()
            w_copy(6, w, j).wait_recv()
        gated(CHUNKS + j, tok)
        to_tokens(CHUNKS + j)
        if j in (1, 2):
            finish_dw(j - 1)

    outs, stage = (y_out, dx_out), (y_st, dx_st)

    def out_copy(i, r):
        return remote(stage[i].at[:, col(r)], outs[i].at[rows_of(OWN), :], out_send.at[i, r], out_recv.at[i, r], dev[r])

    def own_out(i):
        return pltpu.make_async_copy(stage[i].at[:, col(OWN)], outs[i].at[rows_of(OWN), :], lc_out.at[i])

    def y_rows(k, carry):
        rows = pl.ds(pl.multiple_of(k * LN_ROWS, LN_ROWS), LN_ROWS)
        y_st[rows, :] = (xg[rows, :].astype(F32) + m_acc[rows, :]).astype(BF16)
        return carry

    def dx_rows(k, dg):
        rows = pl.ds(pl.multiple_of(k * LN_ROWS, LN_ROWS), LN_ROWS)
        _, xhat, inv = norm(rows)
        dh = dh_acc[rows, :]
        e = dh * gain
        me = jnp.sum(e, axis=1, keepdims=True) * (1.0 / d)
        mex = jnp.sum(e * xhat, axis=1, keepdims=True) * (1.0 / d)
        dx_st[rows, :] = (dyg[rows, :].astype(F32) + inv * (e - me - xhat * mex)).astype(BF16)
        return dg + jnp.sum(dh * xhat, axis=0, keepdims=True)

    lax.fori_loop(0, tok // LN_ROWS, y_rows, 0)
    for r in (NEAR, DIAG, PAIR):
        out_copy(0, r).start()
    own_out(0).start()
    dg = lax.fori_loop(0, tok // LN_ROWS, dx_rows, jnp.zeros((1, d), F32))
    for b in range(4):
        dg_st[b] = dg[:, b * wid:(b + 1) * wid]
    for r in (NEAR, DIAG, PAIR):
        out_copy(1, r).start()
    own_out(1).start()

    def dg_copy(a, r):
        ya = (y, 1 - y)[a]
        return remote(dg_st.at[peer_t[r]], dg_in.at[a, r], dg_send.at[a, r], dg_recv.at[a, r], (ya, peer_t[r]))

    dg_peers = [(a, r) for a in range(2) for r in range(4) if (a, r) != (0, OWN)]
    for a, r in dg_peers:
        dg_copy(a, r).start()

    finish_dw(CHUNKS - 2)
    finish_dw(CHUNKS - 1)

    total_dg = dg_st[t]
    for a, r in dg_peers:
        dg_copy(a, r).wait_recv()
        total_dg = total_dg + dg_in[a, r]
    dg_out[...] = total_dg

    for i in range(2):
        own_out(i).wait()
        for r in (PAIR, NEAR, DIAG):
            in_copy(i, r).wait_send()
            out_copy(i, r).wait_send()
            out_copy(i, r).wait_recv()
        for r in range(4):
            fw_copy(i, r).wait_send()
    for r in (PAIR, NEAR, DIAG):
        g_copy(r).wait_send()
    for a, r in dg_peers:
        dg_copy(a, r).wait_send()
    for j in range(CHUNKS):
        for kind in range(7):
            for w in range(3):
                w_copy(kind, w, j).wait_send()
        pair_copy(0, j).wait_send()
        pair_copy(1, j).wait_send()
        link_copy(j).wait_send()
        for cp in dw_outs(j):
            cp.wait()


def solution(mesh):
    def local_step(x_blk, dy_blk, gain_blk, w_gate_blk, w_up_blk, w_down_blk):
        rows, wid = x_blk.shape
        f = w_gate_blk.shape[1]
        tok, d, fc = rows // 4, 4 * wid, f // CHUNKS
        vm, dma = pltpu.VMEM, pltpu.SemaphoreType.DMA
        any_spec = pl.BlockSpec(memory_space=pl.ANY)
        outs = pl.pallas_call(
            kernel,
            name="mlp_branch",
            out_shape=(jax.ShapeDtypeStruct((rows, wid), BF16), jax.ShapeDtypeStruct((rows, wid), BF16),
                       jax.ShapeDtypeStruct((wid, f), F32), jax.ShapeDtypeStruct((wid, f), F32),
                       jax.ShapeDtypeStruct((f, wid), F32), jax.ShapeDtypeStruct((1, wid), F32)),
            in_specs=[any_spec] * 6,
            out_specs=(any_spec,) * 5 + (pl.BlockSpec(memory_space=pltpu.VMEM),),
            scratch_shapes=[
                vm((2 * tok, d), BF16), vm((2 * tok, d), BF16), vm((4, 1, wid), F32),
                vm((2 * CHUNKS, d, fc), BF16), vm((2 * CHUNKS, d, fc), BF16), vm((2 * CHUNKS, fc, d), BF16),
                vm((2 * tok, d), BF16), vm((d, 2 * tok), BF16), vm((d, 2 * tok), BF16),
                vm((2 * tok, fc), BF16), vm((2 * tok, fc), BF16), vm((2 * tok, fc), BF16),
                vm((CHUNKS, 4, 3 * wid, fc), F32), vm((2, CHUNKS, 3 * wid, fc), F32),
                vm((CHUNKS, 3 * wid, fc), F32), vm((CHUNKS, 3 * wid, fc), F32),
                vm((tok, d), F32), vm((tok, d), F32), vm((tok, d), BF16), vm((tok, d), BF16),
                vm((CHUNKS, 2, wid, fc), F32), vm((CHUNKS, fc, wid), F32),
                vm((4, 1, wid), F32), vm((2, 4, 1, wid), F32),
                dma((4,)), dma((4,)), dma((2, 4)), dma((2, 4)), dma((2, 4)), dma((2, 4)),
                dma((7, 3, CHUNKS)), dma((7, 3, CHUNKS)), dma((2, CHUNKS)), dma((2, CHUNKS)),
                dma((CHUNKS,)), dma((CHUNKS,)), dma((2, 4)), dma((2, 4)), dma((2, 4)), dma((2, 4)),
                dma((2,)), dma((3, CHUNKS)), dma(()), dma((2,)), dma((3, CHUNKS)),
            ],
            compiler_params=pltpu.CompilerParams(collective_id=0, has_side_effects=True,
                                                 vmem_limit_bytes=60 * 2 ** 20),
        )(x_blk, dy_blk, gain_blk.reshape(1, wid), w_gate_blk, w_up_blk, w_down_blk)
        return outs[:5] + (outs[5].reshape(wid),)

    return jax.shard_map(
        local_step, mesh=mesh,
        in_specs=(P("ty", "tx"), P("ty", "tx"), P("tx"), P("tx", "ty"), P("tx", "ty"), P("ty", "tx")),
        out_specs=(P("ty", "tx"), P("ty", "tx"), P("tx", "ty"), P("tx", "ty"), P("ty", "tx"), P("tx")),
        check_vma=False)
```

time: 679 us -> 92.2 us (0.14)
  waiting for transfers between devices: 553 us -> 0 us
  Pallas kernels: 0 us -> 84.3 us
  matrix products: 60.9 us -> 0 us
  blocking collectives: 29.4 us -> 0 us
  other arithmetic: 19 us -> 0 us
  between operations: 14.3 us -> 0.66 us
    reduce_scatter x5 -> x0, waiting for transfers between devices: 376 us -> none  [the longest x1 121 us: local_step(): lax.psum_scatter(jnp.dot(h_all, w_gate_blk, preferred_element_type=jnp.fl...]
    all_gather x5 -> x0, waiting for transfers between devices: 175 us -> none  [the longest x1 54.2 us: local_step(): d_gate_all = lax.all_gather(d_gate, 'tx', axis=0, tiled=True)]
    pallas_call x0 -> x1, Pallas kernels: none -> 84.3 us  [local_step(): pl.pallas_call(kernel, name='mlp_branch', out_shape=(jax.ShapeDtypeStruct...]
    dot_general x9 -> x0, matrix products: 60.9 us -> none  [the longest x3 22.1 us: contract_cols(): lax.dot_general(left_op, right_op, (((1,), (1,)), ((), ())), preferred_el...]
    psum x3 -> x0, blocking collectives: 29.4 us -> none  [the longest x1 13.1 us: local_step(): lax.psum(jnp.stack([jnp.sum(x_float, axis=1), jnp.sum(x_float * x_float,...]
    convert_element_type x3 -> x0, other arithmetic: 15 us -> none  [the longest x1 8.43 us: local_step(): d_up = (d_act * gate_swish).astype(jnp.bfloat16)]
  transfers between devices with their start and end apart: 10 -> 0, of which waited for: 10 -> 0; matrix products, arithmetic and copies ran while one was open for 9% -> 0% of each run, Pallas kernels for 0% -> 0%
where the time goes in v1:
time: 92.2 us; the launch traced here: 91.9 us
  Pallas kernels  84.3 us (91%)
  local copies, waits for them, and re-layouts  6.93 us (8%)
    pallas_call x1, Pallas kernels, local_step(): pl.pallas_call(kernel, name='mlp_branch', out_shape=(jax.ShapeDtypeStruct...  84.3 us
    unnamed x16, local copies, waits for them, and re-layouts  6.93 us

profile of v1, /device:TPU:0, one launch (start us, length us, event | category | flops | bytes accessed | tf_op | source)
XLA Modules:
  0.0 91.9 jit_solution(1057680810555795799)
XLA Ops:
  0.6 84.3 %mlp_branch.1 = (bf16[2048,128]{1,0:T(8,128)(2,1)}, bf16[2048,128]{1,0:T(8,128)(2,1)}, f32[128,1024]{1,0:T(8,128)}, f32[128,1024]{1,0:T(8,128)}, f32[1024,128]{1,0:T(8,128)}, /*index=5*/f32[1,128]{1,0:T(1,128)}) custom-call(bf16[2048,128]{1,0:T(8,128)(2,1)} %x_in.1, bf16[2048,128]{1,0:T(8,128)(2,1)} %dy_in.1, f32[1,128]{1,0:T(1,128)} %bitcast.2, ...), custom_call_target="tpu_custom_call" | custom-call | tf_op jit(solution)/shard_map/mlp_branch/pallas_call | solution.py:350
  84.9 0.0 copy-start.3
  84.9 1.9 %copy.18 = bf16[2048,128]{1,0:T(8,128)(2,1)} copy(bf16[2048,128]{1,0:T(8,128)(2,1)} %get-tuple-element.24) | data formatting | bytes 1048576
  86.9 0.0 copy-done.3
  86.9 0.0 copy-start.2
  86.9 0.8 copy.19
  87.7 0.4 copy-done.2
  88.1 0.0 copy-start.1
  88.1 0.8 copy.20
  88.9 0.4 copy-done.1
  89.3 0.0 copy-start
  89.3 0.8 copy.21
  90.1 0.4 copy-done
  90.6 0.0 copy-start.4
  90.6 0.8 copy.22
  91.4 0.0 copy-done.4
  91.4 0.5 copy.23
Async XLA Ops:
  84.9 1.9 %copy-start.3 = (bf16[2048,128]{1,0:T(8,128)(2,1)S(1)}, bf16[2048,128]{1,0:T(8,128)(2,1)}, u32[]{:S(2)}) copy-start(bf16[2048,128]{1,0:T(8,128)(2,1)} %get-tuple-element.25) | copy-start | bytes 1572868
  86.9 1.2 %copy-start.2 = (f32[128,1024]{1,0:T(8,128)S(1)}, f32[128,1024]{1,0:T(8,128)}, u32[]{:S(2)}) copy-start(f32[128,1024]{1,0:T(8,128)} %get-tuple-element.26) | copy-start | bytes 1572868
  88.1 1.2 %copy-start.1 = (f32[128,1024]{1,0:T(8,128)S(1)}, f32[128,1024]{1,0:T(8,128)}, u32[]{:S(2)}) copy-start(f32[128,1024]{1,0:T(8,128)} %get-tuple-element.27) | copy-start | bytes 1572868
  89.3 1.2 %copy-start = (f32[1024,128]{1,0:T(8,128)S(1)}, f32[1024,128]{1,0:T(8,128)}, u32[]{:S(2)}) copy-start(f32[1024,128]{1,0:T(8,128)} %get-tuple-element.28) | copy-start | bytes 1572868
  90.6 0.8 copy-start.4

commit v2 on v0

v2 whole, which is shorter than its diff:
```python
import jax
import jax.numpy as jnp
from jax import lax
from jax.experimental import pallas as pl
from jax.experimental.pallas import tpu as pltpu
from jax.sharding import PartitionSpec as P

LN_EPS = 1e-6
MESH = pl.DeviceIdType.MESH
F32 = jnp.float32
BF16 = jnp.bfloat16

OWN, PAIR, NEAR, DIAG = 0, 1, 2, 3
CHUNKS = 4
LN_ROWS = 128
ROW_TILE = 256


def dot(a, b):
    return lax.dot_general(a, b, (((1,), (0,)), ((), ())), preferred_element_type=F32)


def dot_nt(a, b):
    return lax.dot_general(a, b, (((1,), (1,)), ((), ())), preferred_element_type=F32)


def kernel(x_in, dy_in, g_in, w1_in, w3_in, w2_in,
           y_out, dx_out, dw1_out, dw3_out, dw2_out, dg_out,
           xg, dyg, gg, w1g, w3g, w2g, h, h_t, dy_t, act, du, dv, part, pair_in, summed, link_in,
           m_acc, dh_acc, y_st, dx_st, dw_st, dw2_st, dg_st, dg_in, st_own, st_in,
           g_send, g_recv, in_send, in_recv, w_send, w_recv, dw_send, dw_recv,
           lk_send, lk_recv, out_send, out_recv, dg_send, dg_recv, st_send, st_recv, lc_in, lc_w, lc_g, lc_out, lc_dw):
    y, t = lax.axis_index("ty"), lax.axis_index("tx")
    x, c = t // 2, t % 2
    tok = x_in.shape[0] // 2
    wid = x_in.shape[1]
    fc = w1_in.shape[1] // CHUNKS
    d = 4 * wid
    half = 2 * wid
    peer_t = (t, 2 * x + 1 - c, 2 * (1 - x) + c, 2 * (1 - x) + 1 - c)
    peer_c = (c, 1 - c, c, 1 - c)
    dev = {r: (y, peer_t[r]) for r in (PAIR, NEAR, DIAG)}
    cross, cross_pair = (1 - y, t), (1 - y, peer_t[PAIR])

    barrier = pltpu.get_barrier_semaphore()
    for to in (dev[PAIR], dev[NEAR], dev[DIAG], cross, cross_pair):
        pl.semaphore_signal(barrier, inc=1, device_id=to, device_id_type=MESH)
    pl.semaphore_wait(barrier, 5)

    def remote(src, dst, send, recv, to):
        return pltpu.make_async_remote_copy(src_ref=src, dst_ref=dst, send_sem=send, recv_sem=recv,
                                            device_id=to, device_id_type=MESH)

    def col(r):
        return pl.ds(pl.multiple_of(peer_t[r] * wid, wid), wid)

    def rows_of(core):
        return pl.ds(pl.multiple_of(core * tok, tok), tok)

    chip = pl.ds(pl.multiple_of(x * half, half), half)
    tin, tg = (x_in, dy_in), (xg, dyg)

    def in_copy(i, r):
        return remote(tin[i].at[rows_of(peer_c[r]), :], tg[i].at[:, col(OWN)], in_send.at[i, r], in_recv.at[i, r], dev[r])

    def own_copy(i):
        return pltpu.make_async_copy(tin[i].at[rows_of(c), :], tg[i].at[:, col(OWN)], lc_in.at[i])

    def g_copy(r):
        return remote(g_in, gg.at[t], g_send.at[r], g_recv.at[r], dev[r])

    def w_src(w, j):
        if w == 2:
            return w2_in.at[pl.ds(j * fc, fc), :]
        return (w1_in, w3_in)[w].at[:, pl.ds(j * fc, fc)]

    def w_dst(w, j, r):
        if w == 2:
            return w2g.at[j, :, col(r)]
        return (w1g, w3g)[w].at[j, col(r), :]

    def w_copy(kind, w, j):
        if kind == 0:
            src, dst, to = w_src(w, j), w_dst(w, j, OWN), dev[NEAR]
        elif kind == 1:
            src, dst, to = w_src(w, j), w_dst(w, j, OWN), dev[PAIR]
        elif kind == 2:
            src, dst, to = w_dst(w, j, NEAR), w_dst(w, j, NEAR), dev[PAIR]
        elif kind == 3:
            src, dst, to = w_src(w, j), w_dst(w, CHUNKS + j, OWN), cross
        elif kind == 4:
            src, dst, to = w_dst(w, CHUNKS + j, OWN), w_dst(w, CHUNKS + j, OWN), dev[NEAR]
        elif kind == 5:
            src, dst, to = w_dst(w, CHUNKS + j, OWN), w_dst(w, CHUNKS + j, OWN), dev[PAIR]
        else:
            src, dst, to = w_dst(w, CHUNKS + j, NEAR), w_dst(w, CHUNKS + j, NEAR), dev[PAIR]
        return remote(src, dst, w_send.at[kind, w, j], w_recv.at[kind, w, j], to)

    def own_w(w, j):
        return pltpu.make_async_copy(w_src(w, j), w_dst(w, j, OWN), lc_w.at[w, j])

    for i in range(2):
        for r in (NEAR, DIAG):
            in_copy(i, r).start()
    for j in range(CHUNKS):
        for w in range(3):
            w_copy(3, w, j).start()
    for i in range(2):
        in_copy(i, PAIR).start()
        own_copy(i).start()
    for r in (PAIR, NEAR, DIAG):
        g_copy(r).start()
    own_g = pltpu.make_async_copy(g_in, gg.at[t], lc_g)
    own_g.start()
    for j in range(CHUNKS):
        for w in range(3):
            w_copy(1, w, j).start()
            own_w(w, j).start()

    def pass_cross(j):
        for w in range(3):
            w_copy(3, w, j).wait_recv()
            w_copy(4, w, j).start()
            w_copy(5, w, j).start()

    pass_cross(0)
    pass_cross(1)
    own_copy(0).wait()
    own_g.wait()
    for r in (PAIR, NEAR, DIAG):
        in_copy(0, r).wait_recv()
        g_copy(r).wait_recv()
    gain = jnp.concatenate([gg[k] for k in range(4)], axis=1)
    gain_chip = jnp.concatenate([gg[2 * x], gg[2 * x + 1]], axis=1)

    def stats(rows):
        xf = xg[rows, :].astype(F32)
        mu = jnp.sum(xf, axis=1, keepdims=True) * (1.0 / d)
        s = jnp.sum(xf * xf, axis=1, keepdims=True) * (1.0 / d)
        return xf, mu, lax.rsqrt(s - mu * mu + LN_EPS)

    def blocks(n, body, carry=0):
        def step(k, carry):
            return body(k, pl.ds(pl.multiple_of(k * n, n), n), carry)
        return lax.fori_loop(0, tok // n, step, carry)

    def ln_rows(k, rows, carry):
        xf, mu, inv = stats(rows)
        h[rows, :] = (gain * ((xf - mu) * inv)).astype(BF16)
        h_t[:, rows] = h[rows, chip].astype(F32).T.astype(BF16)
        return carry

    def dy_rows(k, rows, carry):
        dy_t[:, rows] = dyg[rows, chip].astype(F32).T.astype(BF16)
        return carry

    blocks(LN_ROWS, ln_rows)
    m_acc[...] = jnp.zeros_like(m_acc)
    dh_acc[...] = jnp.zeros_like(dh_acc)
    for j in range(2, CHUNKS):
        pass_cross(j)
    for j in range(CHUNKS):
        for w in range(3):
            w_copy(0, w, j).start()
    own_copy(1).wait()
    for r in (PAIR, NEAR, DIAG):
        in_copy(1, r).wait_recv()
    blocks(LN_ROWS, dy_rows)

    def gated(j):
        def body(k, rows, carry):
            hr = h[rows, :]
            u = dot(hr, w1g[j])
            v = dot(hr, w3g[j])
            da = dot_nt(dyg[rows, :], w2g[j])
            sig = 1.0 / (1.0 + jnp.exp(-u))
            swish = u * sig
            act[rows, :] = (swish * v).astype(BF16)
            du[rows, :] = (da * v * sig * (1.0 + u * (1.0 - sig))).astype(BF16)
            dv[rows, :] = (da * swish).astype(BF16)
            return carry
        blocks(ROW_TILE, body)

    def weight_grads(j):
        for k, (left, right) in enumerate(((h_t, du), (h_t, dv), (dy_t, act))):
            full = dot(left[...], right[...])
            for b in range(2):
                part[j, b, k * wid:(k + 1) * wid, :] = full[b * wid:(b + 1) * wid, :]

    def to_tokens(j):
        def body(k, rows, carry):
            m_acc[rows, :] += dot(act[rows, :], w2g[j, :, chip])
            dh_acc[rows, :] += dot_nt(du[rows, :], w1g[j, chip, :]) + dot_nt(dv[rows, :], w3g[j, chip, :])
            return carry
        blocks(ROW_TILE, body)

    def pair_copy(j):
        return remote(part.at[j, 1 - c], pair_in.at[j], dw_send.at[j], dw_recv.at[j], dev[PAIR])

    def link_copy(j):
        return remote(summed.at[j], link_in.at[j], lk_send.at[j], lk_recv.at[j], cross)

    for j in range(CHUNKS):
        for w in range(3):
            w_copy(4, w, j).wait_recv()
            w_copy(6, w, j).start()
        for w in range(3):
            w_copy(5, w, j).wait_recv()
            w_copy(6, w, j).wait_recv()
        gated(CHUNKS + j)
        weight_grads(CHUNKS + j)
        pair_copy(CHUNKS + j).start()
        to_tokens(CHUNKS + j)
        pair_copy(CHUNKS + j).wait_recv()
        summed[j] = part[CHUNKS + j, c] + pair_in[CHUNKS + j]
        link_copy(j).start()

    for j in range(CHUNKS):
        for w in range(3):
            w_copy(0, w, j).wait_recv()
            w_copy(2, w, j).start()
        for w in range(3):
            own_w(w, j).wait()
            w_copy(1, w, j).wait_recv()
            w_copy(2, w, j).wait_recv()
        gated(j)
        weight_grads(j)
        pair_copy(j).start()
        to_tokens(j)

    outs, stage = (y_out, dx_out), (y_st, dx_st)

    def part_cols(core):
        return pl.ds(pl.multiple_of(core * wid, wid), wid)

    def out_copy(i):
        return remote(stage[i].at[:, part_cols(1 - c)], outs[i].at[rows_of(c), :], out_send.at[i], out_recv.at[i], dev[PAIR])

    def own_out(i):
        return pltpu.make_async_copy(stage[i].at[:, part_cols(c)], outs[i].at[rows_of(c), :], lc_out.at[i])

    lane = lax.broadcasted_iota(jnp.int32, (LN_ROWS, LN_ROWS), 1)

    def sum_rows(k, rows, dg):
        _, mu, inv = stats(rows)
        xhat = (xg[rows, chip].astype(F32) - mu) * inv
        dh = dh_acc[rows, :]
        e = dh * gain_chip
        se = jnp.sum(e, axis=1, keepdims=True)
        sex = jnp.sum(e * xhat, axis=1, keepdims=True)
        st_own[k] = jnp.where(lane == 0, se, jnp.where(lane == 1, sex, 0.0)).T[:8, :]
        return dg + jnp.sum(dh * xhat, axis=0, keepdims=True)

    dg = blocks(LN_ROWS, sum_rows, jnp.zeros((1, half), F32))
    st_copy = remote(st_own, st_in, st_send, st_recv, dev[NEAR])
    st_copy.start()

    def y_rows(k, rows, carry):
        y_st[rows, :] = (xg[rows, chip].astype(F32) + m_acc[rows, :]).astype(BF16)
        return carry

    blocks(LN_ROWS, y_rows)
    out_copy(0).start()
    own_out(0).start()
    for b in range(2):
        dg_st[b] = dg[:, b * wid:(b + 1) * wid]
    dg_copies = [remote(dg_st.at[b], dg_in.at[k], dg_send.at[k], dg_recv.at[k], to)
                 for k, (b, to) in enumerate(((1 - c, dev[PAIR]), (c, cross), (1 - c, cross_pair)))]
    for cp in dg_copies:
        cp.start()

    st_copy.wait_recv()

    def dx_rows(k, rows, carry):
        _, mu, inv = stats(rows)
        xhat = (xg[rows, chip].astype(F32) - mu) * inv
        e = dh_acc[rows, :] * gain_chip
        both = jnp.concatenate([st_own[k] + st_in[k], jnp.zeros((LN_ROWS - 8, LN_ROWS), F32)], axis=0).T * (1.0 / d)
        dx = dyg[rows, chip].astype(F32) + inv * (e - both[:, 0:1] - xhat * both[:, 1:2])
        dx_st[rows, :] = dx.astype(BF16)
        return carry

    blocks(LN_ROWS, dx_rows)
    out_copy(1).start()
    own_out(1).start()

    def dw_outs(j):
        cols = pl.ds(j * fc, fc)
        return (pltpu.make_async_copy(dw_st.at[j, 0], dw1_out.at[:, cols], lc_dw.at[0, j]),
                pltpu.make_async_copy(dw_st.at[j, 1], dw3_out.at[:, cols], lc_dw.at[1, j]),
                pltpu.make_async_copy(dw2_st.at[j], dw2_out.at[cols, :], lc_dw.at[2, j]))

    for j in range(CHUNKS):
        pair_copy(j).wait_recv()
        link_copy(j).wait_recv()
        total = part[j, c] + pair_in[j] + link_in[j]
        dw_st[j, 0] = total[:wid, :]
        dw_st[j, 1] = total[wid:2 * wid, :]
        dw2_st[j] = total[2 * wid:, :].T
        for cp in dw_outs(j):
            cp.start()

    total_dg = dg_st[c]
    for k, cp in enumerate(dg_copies):
        cp.wait_recv()
        total_dg = total_dg + dg_in[k]
    dg_out[...] = total_dg

    for i in range(2):
        own_out(i).wait()
        out_copy(i).wait_send()
        out_copy(i).wait_recv()
        for r in (PAIR, NEAR, DIAG):
            in_copy(i, r).wait_send()
    for r in (PAIR, NEAR, DIAG):
        g_copy(r).wait_send()
    for cp in dg_copies:
        cp.wait_send()
    st_copy.wait_send()
    for j in range(CHUNKS):
        for kind in range(7):
            for w in range(3):
                w_copy(kind, w, j).wait_send()
        pair_copy(j).wait_send()
        pair_copy(CHUNKS + j).wait_send()
        link_copy(j).wait_send()
        for cp in dw_outs(j):
            cp.wait()


def solution(mesh):
    def local_step(x_blk, dy_blk, gain_blk, w_gate_blk, w_up_blk, w_down_blk):
        rows, wid = x_blk.shape
        f = w_gate_blk.shape[1]
        tok, d, half, fc = rows // 2, 4 * wid, 2 * wid, f // CHUNKS
        vm, dma = pltpu.VMEM, pltpu.SemaphoreType.DMA
        any_spec = pl.BlockSpec(memory_space=pl.ANY)
        outs = pl.pallas_call(
            kernel,
            name="mlp_branch",
            out_shape=(jax.ShapeDtypeStruct((rows, wid), BF16), jax.ShapeDtypeStruct((rows, wid), BF16),
                       jax.ShapeDtypeStruct((wid, f), F32), jax.ShapeDtypeStruct((wid, f), F32),
                       jax.ShapeDtypeStruct((f, wid), F32), jax.ShapeDtypeStruct((1, wid), F32)),
            in_specs=[any_spec] * 6,
            out_specs=(any_spec,) * 5 + (pl.BlockSpec(memory_space=pltpu.VMEM),),
            scratch_shapes=[
                vm((tok, d), BF16), vm((tok, d), BF16), vm((4, 1, wid), F32),
                vm((2 * CHUNKS, d, fc), BF16), vm((2 * CHUNKS, d, fc), BF16), vm((2 * CHUNKS, fc, d), BF16),
                vm((tok, d), BF16), vm((half, tok), BF16), vm((half, tok), BF16),
                vm((tok, fc), BF16), vm((tok, fc), BF16), vm((tok, fc), BF16),
                vm((2 * CHUNKS, 2, 3 * wid, fc), F32), vm((2 * CHUNKS, 3 * wid, fc), F32),
                vm((CHUNKS, 3 * wid, fc), F32), vm((CHUNKS, 3 * wid, fc), F32),
                vm((tok, half), F32), vm((tok, half), F32), vm((tok, half), BF16), vm((tok, half), BF16),
                vm((CHUNKS, 2, wid, fc), F32), vm((CHUNKS, fc, wid), F32),
                vm((2, 1, wid), F32), vm((3, 1, wid), F32),
                vm((tok // LN_ROWS, 8, LN_ROWS), F32), vm((tok // LN_ROWS, 8, LN_ROWS), F32),
                dma((4,)), dma((4,)), dma((2, 4)), dma((2, 4)),
                dma((7, 3, CHUNKS)), dma((7, 3, CHUNKS)), dma((2 * CHUNKS,)), dma((2 * CHUNKS,)),
                dma((CHUNKS,)), dma((CHUNKS,)), dma((2,)), dma((2,)), dma((3,)), dma((3,)), dma(()), dma(()),
                dma((2,)), dma((3, CHUNKS)), dma(()), dma((2,)), dma((3, CHUNKS)),
            ],
            compiler_params=pltpu.CompilerParams(collective_id=0, has_side_effects=True,
                                                 vmem_limit_bytes=60 * 2 ** 20),
        )(x_blk, dy_blk, gain_blk.reshape(1, wid), w_gate_blk, w_up_blk, w_down_blk)
        return outs[:5] + (outs[5].reshape(wid),)

    return jax.shard_map(
        local_step, mesh=mesh,
        in_specs=(P("ty", "tx"), P("ty", "tx"), P("tx"), P("tx", "ty"), P("tx", "ty"), P("ty", "tx")),
        out_specs=(P("ty", "tx"), P("ty", "tx"), P("tx", "ty"), P("tx", "ty"), P("ty", "tx"), P("tx")),
        check_vma=False)
```

time: 679 us -> 88.4 us (0.13)
  waiting for transfers between devices: 553 us -> 0 us
  Pallas kernels: 0 us -> 80.6 us
  matrix products: 60.9 us -> 0 us
  blocking collectives: 29.4 us -> 0 us
  other arithmetic: 19 us -> 0 us
  between operations: 14.3 us -> 0.66 us
    reduce_scatter x5 -> x0, waiting for transfers between devices: 376 us -> none  [the longest x1 121 us: local_step(): lax.psum_scatter(jnp.dot(h_all, w_gate_blk, preferred_element_type=jnp.fl...]
    all_gather x5 -> x0, waiting for transfers between devices: 175 us -> none  [the longest x1 54.2 us: local_step(): d_gate_all = lax.all_gather(d_gate, 'tx', axis=0, tiled=True)]
    pallas_call x0 -> x1, Pallas kernels: none -> 80.6 us  [local_step(): pl.pallas_call(kernel, name='mlp_branch', out_shape=(jax.ShapeDtypeStruct...]
    dot_general x9 -> x0, matrix products: 60.9 us -> none  [the longest x3 22.1 us: contract_cols(): lax.dot_general(left_op, right_op, (((1,), (1,)), ((), ())), preferred_el...]
    psum x3 -> x0, blocking collectives: 29.4 us -> none  [the longest x1 13.1 us: local_step(): lax.psum(jnp.stack([jnp.sum(x_float, axis=1), jnp.sum(x_float * x_float,...]
    convert_element_type x3 -> x0, other arithmetic: 15 us -> none  [the longest x1 8.43 us: local_step(): d_up = (d_act * gate_swish).astype(jnp.bfloat16)]
  transfers between devices with their start and end apart: 10 -> 0, of which waited for: 10 -> 0; matrix products, arithmetic and copies ran while one was open for 9% -> 0% of each run, Pallas kernels for 0% -> 0%
where the time goes in v2:
time: 88.4 us; the launch traced here: 88.1 us
  Pallas kernels  80.6 us (91%)
  local copies, waits for them, and re-layouts  6.93 us (8%)
    pallas_call x1, Pallas kernels, local_step(): pl.pallas_call(kernel, name='mlp_branch', out_shape=(jax.ShapeDtypeStruct...  80.6 us
    unnamed x16, local copies, waits for them, and re-layouts  6.93 us

profile of v2, /device:TPU:0, one launch (start us, length us, event | category | flops | bytes accessed | tf_op | source)
XLA Modules:
  0.0 88.1 jit_solution(11302228732716836484)
XLA Ops:
  0.6 80.6 %mlp_branch.1 = (bf16[2048,128]{1,0:T(8,128)(2,1)}, bf16[2048,128]{1,0:T(8,128)(2,1)}, f32[128,1024]{1,0:T(8,128)}, f32[128,1024]{1,0:T(8,128)}, f32[1024,128]{1,0:T(8,128)}, /*index=5*/f32[1,128]{1,0:T(1,128)}) custom-call(bf16[2048,128]{1,0:T(8,128)(2,1)} %x_in.1, bf16[2048,128]{1,0:T(8,128)(2,1)} %dy_in.1, f32[1,128]{1,0:T(1,128)} %bitcast.2, ...), custom_call_target="tpu_custom_call" | custom-call | tf_op jit(solution)/shard_map/mlp_branch/pallas_call | solution.py:338
  81.2 0.0 copy-start.3
  81.2 1.9 %copy.18 = bf16[2048,128]{1,0:T(8,128)(2,1)} copy(bf16[2048,128]{1,0:T(8,128)(2,1)} %get-tuple-element.24) | data formatting | bytes 1048576
  83.1 0.0 copy-done.3
  83.1 0.0 copy-start.2
  83.1 0.8 copy.19
  83.9 0.4 copy-done.2
  84.4 0.0 copy-start.1
  84.4 0.8 copy.20
  85.2 0.4 copy-done.1
  85.6 0.0 copy-start
  85.6 0.8 copy.21
  86.4 0.4 copy-done
  86.8 0.0 copy-start.4
  86.8 0.8 copy.22
  87.6 0.0 copy-done.4
  87.6 0.5 copy.23
Async XLA Ops:
  81.2 1.9 %copy-start.3 = (bf16[2048,128]{1,0:T(8,128)(2,1)S(1)}, bf16[2048,128]{1,0:T(8,128)(2,1)}, u32[]{:S(2)}) copy-start(bf16[2048,128]{1,0:T(8,128)(2,1)} %get-tuple-element.25) | copy-start | bytes 1572868
  83.1 1.2 %copy-start.2 = (f32[128,1024]{1,0:T(8,128)S(1)}, f32[128,1024]{1,0:T(8,128)}, u32[]{:S(2)}) copy-start(f32[128,1024]{1,0:T(8,128)} %get-tuple-element.26) | copy-start | bytes 1572868
  84.4 1.2 %copy-start.1 = (f32[128,1024]{1,0:T(8,128)S(1)}, f32[128,1024]{1,0:T(8,128)}, u32[]{:S(2)}) copy-start(f32[128,1024]{1,0:T(8,128)} %get-tuple-element.27) | copy-start | bytes 1572868
  85.6 1.2 %copy-start = (f32[1024,128]{1,0:T(8,128)S(1)}, f32[1024,128]{1,0:T(8,128)}, u32[]{:S(2)}) copy-start(f32[1024,128]{1,0:T(8,128)} %get-tuple-element.28) | copy-start | bytes 1572868
  86.8 0.8 copy-start.4

commit v3 on v2

v3 whole, which is shorter than its diff:
```python
import jax
import jax.numpy as jnp
from jax import lax
from jax.experimental import pallas as pl
from jax.experimental.pallas import tpu as pltpu
from jax.sharding import PartitionSpec as P

LN_EPS = 1e-6
MESH = pl.DeviceIdType.MESH
F32 = jnp.float32
BF16 = jnp.bfloat16

OWN, PAIR, NEAR, DIAG = 0, 1, 2, 3
EIGHTHS = (1, 2, 2, 2, 1)
CHUNKS = len(EIGHTHS)
LN_ROWS = 128
ROW_TILE = 256


def dot(a, b):
    return lax.dot_general(a, b, (((1,), (0,)), ((), ())), preferred_element_type=F32)


def dot_nt(a, b):
    return lax.dot_general(a, b, (((1,), (1,)), ((), ())), preferred_element_type=F32)


def kernel(x_in, dy_in, g_in, w1_in, w3_in, w2_in,
           y_out, dx_out, dw1_out, dw3_out, dw2_out, dg_out,
           xg, dyg, gg, w1g, w3g, w2g, h, h_t, dy_t, xhat, inv_std, act, du, dv, part, pair_in, summed, link_in,
           m_acc, dh_acc, y_st, dx_st, dg_st, dg_in, st_own, st_in,
           g_send, g_recv, in_send, in_recv, w_send, w_recv, dw_send, dw_recv,
           lk_send, lk_recv, out_send, out_recv, dg_send, dg_recv, st_send, st_recv, lc_in, lc_w, lc_g):
    y, t = lax.axis_index("ty"), lax.axis_index("tx")
    x, c = t // 2, t % 2
    tok = x_in.shape[0] // 2
    wid = x_in.shape[1]
    d = 4 * wid
    half = 2 * wid
    unit = w1_in.shape[1] // 8
    size = [e * unit for e in EIGHTHS]
    start = [sum(size[:i]) for i in range(CHUNKS)]
    span = [pl.ds(start[i], size[i]) for i in range(CHUNKS)]
    peer_t = (t, 2 * x + 1 - c, 2 * (1 - x) + c, 2 * (1 - x) + 1 - c)
    peer_c = (c, 1 - c, c, 1 - c)
    dev = {r: (y, peer_t[r]) for r in (PAIR, NEAR, DIAG)}
    cross, cross_pair = (1 - y, t), (1 - y, peer_t[PAIR])

    barrier = pltpu.get_barrier_semaphore()
    for to in (dev[PAIR], dev[NEAR], dev[DIAG], cross, cross_pair):
        pl.semaphore_signal(barrier, inc=1, device_id=to, device_id_type=MESH)
    pl.semaphore_wait(barrier, 5)

    def remote(src, dst, send, recv, to):
        return pltpu.make_async_remote_copy(src_ref=src, dst_ref=dst, send_sem=send, recv_sem=recv,
                                            device_id=to, device_id_type=MESH)

    def col(r):
        return pl.ds(pl.multiple_of(peer_t[r] * wid, wid), wid)

    def rows_of(core):
        return pl.ds(pl.multiple_of(core * tok, tok), tok)

    def core_cols(core):
        return pl.ds(pl.multiple_of(core * wid, wid), wid)

    chip = pl.ds(pl.multiple_of(x * half, half), half)
    tin, tg = (x_in, dy_in), (xg, dyg)

    def in_copy(i, r):
        return remote(tin[i].at[rows_of(peer_c[r]), :], tg[i].at[:, col(OWN)], in_send.at[i, r], in_recv.at[i, r], dev[r])

    def own_copy(i):
        return pltpu.make_async_copy(tin[i].at[rows_of(c), :], tg[i].at[:, col(OWN)], lc_in.at[i])

    def g_copy(r):
        return remote(g_in, gg.at[t], g_send.at[r], g_recv.at[r], dev[r])

    def w_src(w, j):
        if w == 2:
            return w2_in.at[span[j], :]
        return (w1_in, w3_in)[w].at[:, span[j]]

    def w_dst(w, side, j, r):
        if w == 2:
            return w2g.at[side, span[j], col(r)]
        return (w1g, w3g)[w].at[side, col(r), span[j]]

    def w_copy(kind, w, j):
        if kind == 0:
            src, dst, to = w_src(w, j), w_dst(w, 0, j, OWN), dev[NEAR]
        elif kind == 1:
            src, dst, to = w_src(w, j), w_dst(w, 0, j, OWN), dev[PAIR]
        elif kind == 2:
            src, dst, to = w_dst(w, 0, j, NEAR), w_dst(w, 0, j, NEAR), dev[PAIR]
        elif kind == 3:
            src, dst, to = w_src(w, j), w_dst(w, 1, j, OWN), cross
        elif kind == 4:
            src, dst, to = w_dst(w, 1, j, OWN), w_dst(w, 1, j, OWN), dev[NEAR]
        elif kind == 5:
            src, dst, to = w_dst(w, 1, j, OWN), w_dst(w, 1, j, OWN), dev[PAIR]
        else:
            src, dst, to = w_dst(w, 1, j, NEAR), w_dst(w, 1, j, NEAR), dev[PAIR]
        return remote(src, dst, w_send.at[kind, w, j], w_recv.at[kind, w, j], to)

    def own_w(w, j):
        return pltpu.make_async_copy(w_src(w, j), w_dst(w, 0, j, OWN), lc_w.at[w, j])

    for i in range(2):
        for r in (NEAR, DIAG):
            in_copy(i, r).start()
    for j in range(CHUNKS):
        for w in range(3):
            w_copy(3, w, j).start()
    for i in range(2):
        in_copy(i, PAIR).start()
        own_copy(i).start()
    for r in (PAIR, NEAR, DIAG):
        g_copy(r).start()
    own_g = pltpu.make_async_copy(g_in, gg.at[t], lc_g)
    own_g.start()
    for j in range(CHUNKS):
        for w in range(3):
            w_copy(1, w, j).start()
            own_w(w, j).start()

    def pass_cross(j):
        for w in range(3):
            w_copy(3, w, j).wait_recv()
            w_copy(4, w, j).start()
            w_copy(5, w, j).start()

    pass_cross(0)
    pass_cross(1)
    own_copy(0).wait()
    own_g.wait()
    for r in (PAIR, NEAR, DIAG):
        in_copy(0, r).wait_recv()
        g_copy(r).wait_recv()
    gain = jnp.concatenate([gg[k] for k in range(4)], axis=1)
    gain_chip = jnp.concatenate([gg[2 * x], gg[2 * x + 1]], axis=1)

    def blocks(n, body, carry=0, lo=0, hi=None):
        def step(k, carry):
            return body(k, pl.ds(pl.multiple_of(k * n, n), n), carry)
        return lax.fori_loop(lo // n, (tok if hi is None else hi) // n, step, carry)

    def ln_rows(k, rows, carry):
        xf = xg[rows, :].astype(F32)
        mu = jnp.sum(xf, axis=1, keepdims=True) * (1.0 / d)
        s = jnp.sum(xf * xf, axis=1, keepdims=True) * (1.0 / d)
        inv = lax.rsqrt(s - mu * mu + LN_EPS)
        xh = (xf - mu) * inv
        xhat[rows, :] = xh
        inv_std[rows, :] = inv
        h[rows, :] = (gain * xh).astype(BF16)
        h_t[:, rows] = h[rows, chip].astype(F32).T.astype(BF16)
        return carry

    def dy_rows(k, rows, carry):
        dy_t[:, rows] = dyg[rows, chip].astype(F32).T.astype(BF16)
        return carry

    blocks(LN_ROWS, ln_rows)
    for j in range(2, CHUNKS):
        pass_cross(j)
    for j in range(CHUNKS):
        for w in range(3):
            w_copy(0, w, j).start()
    own_copy(1).wait()
    for r in (PAIR, NEAR, DIAG):
        in_copy(1, r).wait_recv()
    blocks(LN_ROWS, dy_rows)

    def gated(s, j):
        n = size[j]

        def body(k, rows, carry):
            hr = h[rows, :]
            u = dot(hr, w1g[s, :, span[j]])
            v = dot(hr, w3g[s, :, span[j]])
            da = dot_nt(dyg[rows, :], w2g[s, span[j], :])
            sig = 1.0 / (1.0 + jnp.exp(-u))
            swish = u * sig
            act[rows, :n] = (swish * v).astype(BF16)
            du[rows, :n] = (da * v * sig * (1.0 + u * (1.0 - sig))).astype(BF16)
            dv[rows, :n] = (da * swish).astype(BF16)
            return carry
        blocks(ROW_TILE, body)

    def pair_copy(s, j, k):
        band = pl.ds(k * wid, wid)
        return remote(part.at[s, 1 - c, band, span[j]], pair_in.at[s, band, span[j]],
                      dw_send.at[s, j, k], dw_recv.at[s, j, k], dev[PAIR])

    def weight_grads(s, j):
        for k, (left, right) in enumerate(((h_t, du), (h_t, dv), (dy_t, act))):
            full = dot(left[...], right[:, :size[j]])
            for b in range(2):
                part[s, b, k * wid:(k + 1) * wid, span[j]] = full[b * wid:(b + 1) * wid, :]
            pair_copy(s, j, k).start()

    def link_copy(j, k):
        band = pl.ds(k * wid, wid)
        return remote(summed.at[band, span[j]], link_in.at[band, span[j]], lk_send.at[j, k], lk_recv.at[j, k], cross)

    def send_sums(j):
        for k in range(3):
            band = pl.ds(k * wid, wid)
            pair_copy(1, j, k).wait_recv()
            summed[band, span[j]] = part[1, c, band, span[j]] + pair_in[1, band, span[j]]
            link_copy(j, k).start()

    def token_sums(s, j, rows):
        n = size[j]
        m = dot(act[rows, :n], w2g[s, span[j], chip])
        dh = dot_nt(du[rows, :n], w1g[s, chip, span[j]]) + dot_nt(dv[rows, :n], w3g[s, chip, span[j]])
        return m, dh

    def to_tokens(s, j, first=False):
        def body(k, rows, carry):
            m, dh = token_sums(s, j, rows)
            if first:
                m_acc[rows, :] = m
                dh_acc[rows, :] = dh
            else:
                m_acc[rows, :] += m
                dh_acc[rows, :] += dh
            return carry
        blocks(ROW_TILE, body)

    def pass_near(kind, j):
        for w in range(3):
            w_copy(kind, w, j).wait_recv()
            w_copy(6 if kind == 4 else 2, w, j).start()

    pass_near(4, 0)
    for j in range(CHUNKS):
        for w in range(3):
            w_copy(5, w, j).wait_recv()
            w_copy(6, w, j).wait_recv()
        gated(1, j)
        weight_grads(1, j)
        if j == 0:
            send_sums(j)
        to_tokens(1, j, first=j == 0)
        if j + 1 < CHUNKS:
            pass_near(4, j + 1)
        else:
            pass_near(0, 0)
        if j:
            send_sums(j)

    def finish_dw(j):
        for k in range(3):
            pair_copy(0, j, k).wait_recv()
            link_copy(j, k).wait_recv()
            band = pl.ds(k * wid, wid)
            total = part[0, c, band, span[j]] + pair_in[0, band, span[j]] + link_in[band, span[j]]
            if k == 2:
                dw2_out[span[j], :] = total.T
            else:
                (dw1_out, dw3_out)[k][:, span[j]] = total

    lane = lax.broadcasted_iota(jnp.int32, (LN_ROWS, LN_ROWS), 1)
    last = CHUNKS - 1

    def last_rows(k, rows, dg):
        m, dh = token_sums(0, last, rows)
        m_acc[rows, :] += m
        dh = dh_acc[rows, :] + dh
        dh_acc[rows, :] = dh
        xh = xhat[rows, chip]
        e = dh * gain_chip
        se = jnp.sum(e, axis=1, keepdims=True)
        sex = jnp.sum(e * xh, axis=1, keepdims=True)
        st_own[k] = jnp.where(lane == 0, se, jnp.where(lane == 1, sex, 0.0)).T[:8, :]
        return dg + jnp.sum(dh * xh, axis=0, keepdims=True)

    for j in range(CHUNKS):
        for w in range(3):
            own_w(w, j).wait()
            w_copy(1, w, j).wait_recv()
            w_copy(2, w, j).wait_recv()
        gated(0, j)
        if j < last:
            weight_grads(0, j)
            to_tokens(0, j)
            pass_near(0, j + 1)
            if j:
                finish_dw(j - 1)

    dg = blocks(LN_ROWS, last_rows, jnp.zeros((1, half), F32))
    st_copy = remote(st_own, st_in, st_send, st_recv, dev[NEAR])
    st_copy.start()
    weight_grads(0, last)

    outs, stage = (y_out, dx_out), (y_st, dx_st)
    mid = tok // 2

    def out_copy(i, part_of):
        rows = pl.ds(part_of * mid, mid)
        to_rows = pl.ds(pl.multiple_of(c * tok + part_of * mid, mid), mid)
        src = y_st.at[rows, :] if i == 0 else dx_st.at[rows, core_cols(1 - c)]
        return remote(src, outs[i].at[to_rows, :], out_send.at[i, part_of], out_recv.at[i, part_of], dev[PAIR])

    def out_rows(k):
        return pl.ds(pl.multiple_of(c * tok + k * LN_ROWS, LN_ROWS), LN_ROWS)

    def y_rows(k, rows, carry):
        y_st[rows, :] = (xg[rows, col(PAIR)].astype(F32) + m_acc[rows, core_cols(1 - c)]).astype(BF16)
        y_out[out_rows(k), :] = (xg[rows, col(OWN)].astype(F32) + m_acc[rows, core_cols(c)]).astype(BF16)
        return carry

    blocks(LN_ROWS, y_rows)
    for b in range(2):
        dg_st[b] = dg[:, b * wid:(b + 1) * wid]
        out_copy(0, b).start()
    dg_copies = [remote(dg_st.at[b], dg_in.at[k], dg_send.at[k], dg_recv.at[k], to)
                 for k, (b, to) in enumerate(((1 - c, dev[PAIR]), (c, cross), (1 - c, cross_pair)))]
    for cp in dg_copies:
        cp.start()

    st_copy.wait_recv()

    def dx_rows(k, rows, carry):
        both = jnp.concatenate([st_own[k] + st_in[k], jnp.zeros((LN_ROWS - 8, LN_ROWS), F32)], axis=0).T * (1.0 / d)
        e = dh_acc[rows, :] * gain_chip
        dx_ln = inv_std[rows, :] * (e - both[:, 0:1] - xhat[rows, chip] * both[:, 1:2])
        dx_st[rows, :] = (dyg[rows, chip].astype(F32) + dx_ln).astype(BF16)
        dx_out[out_rows(k), :] = dx_st[rows, core_cols(c)]
        return carry

    for b in range(2):
        blocks(LN_ROWS, dx_rows, lo=b * mid, hi=(b + 1) * mid)
        out_copy(1, b).start()

    finish_dw(last - 1)
    finish_dw(last)

    total_dg = dg_st[c]
    for k, cp in enumerate(dg_copies):
        cp.wait_recv()
        total_dg = total_dg + dg_in[k]
    dg_out[...] = total_dg

    for i in range(2):
        for b in range(2):
            out_copy(i, b).wait_send()
            out_copy(i, b).wait_recv()
        for r in (PAIR, NEAR, DIAG):
            in_copy(i, r).wait_send()
    for r in (PAIR, NEAR, DIAG):
        g_copy(r).wait_send()
    for cp in dg_copies:
        cp.wait_send()
    st_copy.wait_send()
    for j in range(CHUNKS):
        for k in range(3):
            for kind in range(7):
                w_copy(kind, k, j).wait_send()
            pair_copy(0, j, k).wait_send()
            pair_copy(1, j, k).wait_send()
            link_copy(j, k).wait_send()


def write_out(*refs):
    n = len(refs) // 2
    copies = [pltpu.make_async_copy(refs[i], refs[n + i], refs[2 * n].at[i]) for i in range(n)]
    for cp in copies:
        cp.start()
    for cp in copies:
        cp.wait()


def solution(mesh):
    def local_step(x_blk, dy_blk, gain_blk, w_gate_blk, w_up_blk, w_down_blk):
        rows, wid = x_blk.shape
        f = w_gate_blk.shape[1]
        tok, d, half, fc = rows // 2, 4 * wid, 2 * wid, f // 8 * max(EIGHTHS)
        vm, dma = pltpu.VMEM, pltpu.SemaphoreType.DMA
        in_vmem = pl.BlockSpec(memory_space=pltpu.VMEM)
        args = (x_blk, dy_blk, gain_blk.reshape(1, wid), w_gate_blk, w_up_blk, w_down_blk)
        outs = pl.pallas_call(
            kernel,
            name="mlp_branch",
            out_shape=(jax.ShapeDtypeStruct((rows, wid), BF16), jax.ShapeDtypeStruct((rows, wid), BF16),
                       jax.ShapeDtypeStruct((wid, f), F32), jax.ShapeDtypeStruct((wid, f), F32),
                       jax.ShapeDtypeStruct((f, wid), F32), jax.ShapeDtypeStruct((1, wid), F32)),
            in_specs=[pl.BlockSpec(memory_space=pltpu.HBM)] * 6,
            out_specs=(in_vmem,) * 6,
            scratch_shapes=[
                vm((tok, d), BF16), vm((tok, d), BF16), vm((4, 1, wid), F32),
                vm((2, d, f), BF16), vm((2, d, f), BF16), vm((2, f, d), BF16),
                vm((tok, d), BF16), vm((half, tok), BF16), vm((half, tok), BF16), vm((tok, d), F32), vm((tok, 1), F32),
                vm((tok, fc), BF16), vm((tok, fc), BF16), vm((tok, fc), BF16),
                vm((2, 2, 3 * wid, f), F32), vm((2, 3 * wid, f), F32), vm((3 * wid, f), F32), vm((3 * wid, f), F32),
                vm((tok, half), F32), vm((tok, half), F32), vm((tok, wid), BF16), vm((tok, half), BF16),
                vm((2, 1, wid), F32), vm((3, 1, wid), F32),
                vm((tok // LN_ROWS, 8, LN_ROWS), F32), vm((tok // LN_ROWS, 8, LN_ROWS), F32),
                dma((4,)), dma((4,)), dma((2, 4)), dma((2, 4)),
                dma((7, 3, CHUNKS)), dma((7, 3, CHUNKS)), dma((2, CHUNKS, 3)), dma((2, CHUNKS, 3)),
                dma((CHUNKS, 3)), dma((CHUNKS, 3)), dma((2, 2)), dma((2, 2)), dma((3,)), dma((3,)), dma(()), dma(()),
                dma((2,)), dma((3, CHUNKS)), dma(()),
            ],
            compiler_params=pltpu.CompilerParams(collective_id=0, has_side_effects=True,
                                                 vmem_limit_bytes=44 * 2 ** 20),
        )(*(pltpu.with_memory_space_constraint(a, pltpu.HBM) for a in args))
        outs = pl.pallas_call(
            write_out,
            name="write_out",
            out_shape=tuple(jax.ShapeDtypeStruct(o.shape, o.dtype) for o in outs),
            in_specs=[in_vmem] * 6,
            out_specs=(pl.BlockSpec(memory_space=pl.ANY),) * 6,
            scratch_shapes=[dma((6,))],
            compiler_params=pltpu.CompilerParams(vmem_limit_bytes=2 ** 20),
        )(*outs)
        return outs[:5] + (outs[5].reshape(wid),)

    return jax.shard_map(
        local_step, mesh=mesh,
        in_specs=(P("ty", "tx"), P("ty", "tx"), P("tx"), P("tx", "ty"), P("tx", "ty"), P("ty", "tx")),
        out_specs=(P("ty", "tx"), P("ty", "tx"), P("tx", "ty"), P("tx", "ty"), P("ty", "tx"), P("tx")),
        check_vma=False)
```

time: 88.4 us -> 92.8 us (1.050)
  Pallas kernels: 80.6 us -> 92.1 us
  local copies, waits for them, and re-layouts: 6.93 us -> 0 us
    pallas_call x1, Pallas kernels: 80.6 us -> 90.6 us  [local_step(): pl.pallas_call(kernel, name='mlp_branch', out_shape=(jax.ShapeDtypeStruct...]
    unnamed x16 -> x0, local copies, waits for them, and re-layouts: 6.93 us -> none
    pallas_call x0 -> x1, Pallas kernels: none -> 1.54 us  [local_step(): pl.pallas_call(write_out, name='write_out', out_shape=tuple((jax.ShapeDty...]
where the time goes in v3:
time: 92.8 us; the launch traced here: 92.7 us
  Pallas kernels  92.1 us (99%)
    pallas_call x1, Pallas kernels, local_step(): pl.pallas_call(kernel, name='mlp_branch', out_shape=(jax.ShapeDtypeStruct...  90.6 us

profile of v3, /device:TPU:0, one launch (start us, length us, event | category | flops | bytes accessed | tf_op | source)
XLA Modules:
  0.0 92.7 jit_solution(7301817023933680355)
XLA Ops:
  0.6 90.6 %mlp_branch.1 = (bf16[2048,128]{1,0:T(8,128)(2,1)S(1)}, bf16[2048,128]{1,0:T(8,128)(2,1)S(1)}, f32[128,1024]{1,0:T(8,128)S(1)}, f32[128,1024]{1,0:T(8,128)S(1)},...) custom-call(bf16[2048,128]{1,0:T(8,128)(2,1)} %x_in.1, bf16[2048,128]{1,0:T(8,128)(2,1)} %dy_in.1, f32[1,128]{1,0:T(1,128)} %bitcast.2, ...), custom_call_target="tpu_custom_call" | custom-call | tf_op jit(solution)/shard_map/mlp_branch/pallas_call | solution.py:384
  91.2 1.5 %write_out.1 = (bf16[2048,128]{1,0:T(8,128)(2,1)}, bf16[2048,128]{1,0:T(8,128)(2,1)}, f32[128,1024]{1,0:T(8,128)}, f32[128,1024]{1,0:T(8,128)}, f32[1024,128]{1,0:T(8,128)}, /*index=5*/f32[1,128]{1,0:T(1,128)}) custom-call(bf16[2048,128]{1,0:T(8,128)(2,1)S(1)} %get-tuple-element.18.refs_0_, bf16[2048,128]{1,0:T(8,128)(2,1)S(1)} %get-tuple-element.19.refs_1_, ...), custom_call_target="tpu_custom_call" | custom-call | tf_op jit(solution)/shard_map/write_out/pallas_call | solution.py:409

commit v4 on v3

--- a/solution.py
+++ b/solution.py
@@ -11,7 +11,7 @@
 BF16 = jnp.bfloat16
 
 OWN, PAIR, NEAR, DIAG = 0, 1, 2, 3
-EIGHTHS = (1, 2, 2, 2, 1)
+EIGHTHS = (2, 2, 2, 2)
 CHUNKS = len(EIGHTHS)
 LN_ROWS = 128
 ROW_TILE = 256
@@ -101,11 +101,21 @@
             src, dst, to = w_dst(w, 1, j, OWN), w_dst(w, 1, j, OWN), dev[PAIR]
         else:
             src, dst, to = w_dst(w, 1, j, NEAR), w_dst(w, 1, j, NEAR), dev[PAIR]
-        return remote(src, dst, w_send.at[kind, w, j], w_recv.at[kind, w, j], to)
+        return remote(src, dst, w_send.at[kind], w_recv.at[kind, j], to)
+
+    def w_arrived(kind, j):
+        ref = w1g.at[kind // 3 % 2, pl.ds(0, 3 * wid), span[j]]
+        pltpu.make_async_copy(ref, ref, w_recv.at[kind, j]).wait()
+
+    def w_sent(kind):
+        ref = w1g.at[0, pl.ds(0, 3 * wid), :]
+        pltpu.make_async_copy(ref, ref, w_send.at[kind]).wait()
 
     def own_w(w, j):
-        return pltpu.make_async_copy(w_src(w, j), w_dst(w, 0, j, OWN), lc_w.at[w, j])
-
+        return pltpu.make_async_copy(w_src(w, j), w_dst(w, 0, j, OWN), lc_w)
+
+    for r in (PAIR, NEAR, DIAG):
+        g_copy(r).start()
     for i in range(2):
         for r in (NEAR, DIAG):
             in_copy(i, r).start()
@@ -115,8 +125,6 @@
     for i in range(2):
         in_copy(i, PAIR).start()
         own_copy(i).start()
-    for r in (PAIR, NEAR, DIAG):
-        g_copy(r).start()
     own_g = pltpu.make_async_copy(g_in, gg.at[t], lc_g)
     own_g.start()
     for j in range(CHUNKS):
@@ -125,8 +133,8 @@
             own_w(w, j).start()
 
     def pass_cross(j):
+        w_arrived(3, j)
         for w in range(3):
-            w_copy(3, w, j).wait_recv()
             w_copy(4, w, j).start()
             w_copy(5, w, j).start()
 
@@ -143,7 +151,7 @@
     def blocks(n, body, carry=0, lo=0, hi=None):
         def step(k, carry):
             return body(k, pl.ds(pl.multiple_of(k * n, n), n), carry)
-        return lax.fori_loop(lo // n, (tok if hi is None else hi) // n, step, carry)
+        return lax.fori_loop(lo // n, (tok if hi is None else hi) // n, step, carry, unroll=True)
 
     def ln_rows(k, rows, carry):
         xf = xg[rows, :].astype(F32)
@@ -188,28 +196,22 @@
             return carry
         blocks(ROW_TILE, body)
 
-    def pair_copy(s, j, k):
-        band = pl.ds(k * wid, wid)
-        return remote(part.at[s, 1 - c, band, span[j]], pair_in.at[s, band, span[j]],
-                      dw_send.at[s, j, k], dw_recv.at[s, j, k], dev[PAIR])
+    def pair_copy(s, j):
+        return remote(part.at[s, 1 - c, :, span[j]], pair_in.at[s, :, span[j]], dw_send.at[s, j], dw_recv.at[s, j], dev[PAIR])
 
     def weight_grads(s, j):
         for k, (left, right) in enumerate(((h_t, du), (h_t, dv), (dy_t, act))):
             full = dot(left[...], right[:, :size[j]])
             for b in range(2):
                 part[s, b, k * wid:(k + 1) * wid, span[j]] = full[b * wid:(b + 1) * wid, :]
-            pair_copy(s, j, k).start()
-
-    def link_copy(j, k):
-        band = pl.ds(k * wid, wid)
-        return remote(summed.at[band, span[j]], link_in.at[band, span[j]], lk_send.at[j, k], lk_recv.at[j, k], cross)
+
+    def link_copy(j):
+        return remote(summed.at[:, span[j]], link_in.at[:, span[j]], lk_send.at[j], lk_recv.at[j], cross)
 
     def send_sums(j):
-        for k in range(3):
-            band = pl.ds(k * wid, wid)
-            pair_copy(1, j, k).wait_recv()
-            summed[band, span[j]] = part[1, c, band, span[j]] + pair_in[1, band, span[j]]
-            link_copy(j, k).start()
+        pair_copy(1, j).wait_recv()
+        summed[:, span[j]] = part[1, c, :, span[j]] + pair_in[1, :, span[j]]
+        link_copy(j).start()
 
     def token_sums(s, j, rows):
         n = size[j]
@@ -230,31 +232,34 @@
         blocks(ROW_TILE, body)
 
     def pass_near(kind, j):
+        w_arrived(kind, j)
         for w in range(3):
-            w_copy(kind, w, j).wait_recv()
             w_copy(6 if kind == 4 else 2, w, j).start()
 
     pass_near(4, 0)
     for j in range(CHUNKS):
-        for w in range(3):
-            w_copy(5, w, j).wait_recv()
-            w_copy(6, w, j).wait_recv()
+        w_arrived(5, j)
+        w_arrived(6, j)
+        if j > 1:
+            send_sums(j - 1)
         gated(1, j)
         weight_grads(1, j)
         if j == 0:
+            pair_copy(1, j).start()
+        to_tokens(1, j, first=j == 0)
+        if j:
+            pair_copy(1, j).start()
+        if j == 0:
             send_sums(j)
-        to_tokens(1, j, first=j == 0)
         if j + 1 < CHUNKS:
             pass_near(4, j + 1)
         else:
             pass_near(0, 0)
-        if j:
-            send_sums(j)
 
     def finish_dw(j):
+        pair_copy(0, j).wait_recv()
+        link_copy(j).wait_recv()
         for k in range(3):
-            pair_copy(0, j, k).wait_recv()
-            link_copy(j, k).wait_recv()
             band = pl.ds(k * wid, wid)
             total = part[0, c, band, span[j]] + pair_in[0, band, span[j]] + link_in[band, span[j]]
             if k == 2:
@@ -278,14 +283,17 @@
         return dg + jnp.sum(dh * xh, axis=0, keepdims=True)
 
     for j in range(CHUNKS):
-        for w in range(3):
-            own_w(w, j).wait()
-            w_copy(1, w, j).wait_recv()
-            w_copy(2, w, j).wait_recv()
+        w_arrived(1, j)
+        w_arrived(2, j)
+        if j == 0:
+            send_sums(last)
+            ref = w1g.at[0, pl.ds(0, 3 * wid), :]
+            pltpu.make_async_copy(ref, ref, lc_w).wait()
         gated(0, j)
         if j < last:
             weight_grads(0, j)
             to_tokens(0, j)
+            pair_copy(0, j).start()
             pass_near(0, j + 1)
             if j:
                 finish_dw(j - 1)
@@ -294,6 +302,7 @@
     st_copy = remote(st_own, st_in, st_send, st_recv, dev[NEAR])
     st_copy.start()
     weight_grads(0, last)
+    pair_copy(0, last).start()
 
     outs, stage = (y_out, dx_out), (y_st, dx_st)
     mid = tok // 2
@@ -321,6 +330,18 @@
     for cp in dg_copies:
         cp.start()
 
+    for r in (PAIR, NEAR, DIAG):
+        g_copy(r).wait_send()
+        for i in range(2):
+            in_copy(i, r).wait_send()
+    for kind in range(7):
+        w_sent(kind)
+    for j in range(CHUNKS):
+        pair_copy(1, j).wait_send()
+        if j < last:
+            pair_copy(0, j).wait_send()
+        if j < last - 1:
+            link_copy(j).wait_send()
     st_copy.wait_recv()
 
     def dx_rows(k, rows, carry):
@@ -348,20 +369,12 @@
         for b in range(2):
             out_copy(i, b).wait_send()
             out_copy(i, b).wait_recv()
-        for r in (PAIR, NEAR, DIAG):
-            in_copy(i, r).wait_send()
-    for r in (PAIR, NEAR, DIAG):
-        g_copy(r).wait_send()
     for cp in dg_copies:
         cp.wait_send()
     st_copy.wait_send()
-    for j in range(CHUNKS):
-        for k in range(3):
-            for kind in range(7):
-                w_copy(kind, k, j).wait_send()
-            pair_copy(0, j, k).wait_send()
-            pair_copy(1, j, k).wait_send()
-            link_copy(j, k).wait_send()
+    pair_copy(0, last).wait_send()
+    link_copy(last - 1).wait_send()
+    link_copy(last).wait_send()
 
 
 def write_out(*refs):
@@ -399,9 +412,9 @@
                 vm((2, 1, wid), F32), vm((3, 1, wid), F32),
                 vm((tok // LN_ROWS, 8, LN_ROWS), F32), vm((tok // LN_ROWS, 8, LN_ROWS), F32),
                 dma((4,)), dma((4,)), dma((2, 4)), dma((2, 4)),
-                dma((7, 3, CHUNKS)), dma((7, 3, CHUNKS)), dma((2, CHUNKS, 3)), dma((2, CHUNKS, 3)),
-                dma((CHUNKS, 3)), dma((CHUNKS, 3)), dma((2, 2)), dma((2, 2)), dma((3,)), dma((3,)), dma(()), dma(()),
-                dma((2,)), dma((3, CHUNKS)), dma(()),
+                dma((7,)), dma((7, CHUNKS)), dma((2, CHUNKS)), dma((2, CHUNKS)),
+                dma((CHUNKS,)), dma((CHUNKS,)), dma((2, 2)), dma((2, 2)), dma((3,)), dma((3,)), dma(()), dma(()),
+                dma((2,)), dma(()), dma(()),
             ],
             compiler_params=pltpu.CompilerParams(collective_id=0, has_side_effects=True,
                                                  vmem_limit_bytes=44 * 2 ** 20),

time: 92.8 us -> 75.6 us (0.81)
  Pallas kernels: 92.1 us -> 74.7 us
    pallas_call x1, Pallas kernels: 90.6 us -> 73.2 us  [local_step(): pl.pallas_call(kernel, name='mlp_branch', out_shape=(jax.ShapeDtypeStruct...]
where the time goes in v4:
time: 75.6 us; the launch traced here: 75.5 us
  Pallas kernels  74.7 us (99%)
  between operations  0.8 us (1%)
    pallas_call x1, Pallas kernels, local_step(): pl.pallas_call(kernel, name='mlp_branch', out_shape=(jax.ShapeDtypeStruct...  73.2 us
    pallas_call x1, Pallas kernels, local_step(): pl.pallas_call(write_out, name='write_out', out_shape=tuple((jax.ShapeDty...  1.54 us

profile of v4, /device:TPU:0, one launch (start us, length us, event | category | flops | bytes accessed | tf_op | source)
XLA Modules:
  0.0 75.5 jit_solution(13646204144465122641)
XLA Ops:
  0.6 73.2 %mlp_branch.1 = (bf16[2048,128]{1,0:T(8,128)(2,1)S(1)}, bf16[2048,128]{1,0:T(8,128)(2,1)S(1)}, f32[128,1024]{1,0:T(8,128)S(1)}, f32[128,1024]{1,0:T(8,128)S(1)},...) custom-call(bf16[2048,128]{1,0:T(8,128)(2,1)} %x_in.1, bf16[2048,128]{1,0:T(8,128)(2,1)} %dy_in.1, f32[1,128]{1,0:T(1,128)} %bitcast.2, ...), custom_call_target="tpu_custom_call" | custom-call | tf_op jit(solution)/shard_map/mlp_branch/pallas_call | solution.py:397
  73.8 1.5 %write_out.1 = (bf16[2048,128]{1,0:T(8,128)(2,1)}, bf16[2048,128]{1,0:T(8,128)(2,1)}, f32[128,1024]{1,0:T(8,128)}, f32[128,1024]{1,0:T(8,128)}, f32[1024,128]{1,0:T(8,128)}, /*index=5*/f32[1,128]{1,0:T(1,128)}) custom-call(bf16[2048,128]{1,0:T(8,128)(2,1)S(1)} %get-tuple-element.18.refs_0_, bf16[2048,128]{1,0:T(8,128)(2,1)S(1)} %get-tuple-element.19.refs_1_, ...), custom_call_target="tpu_custom_call" | custom-call | tf_op jit(solution)/shard_map/write_out/pallas_call | solution.py:422

commit v5 on v4

--- a/solution.py
+++ b/solution.py
@@ -28,7 +28,7 @@
 def kernel(x_in, dy_in, g_in, w1_in, w3_in, w2_in,
            y_out, dx_out, dw1_out, dw3_out, dw2_out, dg_out,
            xg, dyg, gg, w1g, w3g, w2g, h, h_t, dy_t, xhat, inv_std, act, du, dv, part, pair_in, summed, link_in,
-           m_acc, dh_acc, y_st, dx_st, dg_st, dg_in, st_own, st_in,
+           m_acc, dh_acc, dh_last, y_st, dx_st, dg_st, dg_in, st_own, st_in,
            g_send, g_recv, in_send, in_recv, w_send, w_recv, dw_send, dw_recv,
            lk_send, lk_recv, out_send, out_recv, dg_send, dg_recv, st_send, st_recv, lc_in, lc_w, lc_g):
     y, t = lax.axis_index("ty"), lax.axis_index("tx")
@@ -101,11 +101,12 @@
             src, dst, to = w_dst(w, 1, j, OWN), w_dst(w, 1, j, OWN), dev[PAIR]
         else:
             src, dst, to = w_dst(w, 1, j, NEAR), w_dst(w, 1, j, NEAR), dev[PAIR]
-        return remote(src, dst, w_send.at[kind], w_recv.at[kind, j], to)
-
-    def w_arrived(kind, j):
-        ref = w1g.at[kind // 3 % 2, pl.ds(0, 3 * wid), span[j]]
-        pltpu.make_async_copy(ref, ref, w_recv.at[kind, j]).wait()
+        slot = CHUNKS if w == 2 and j == 0 and kind in (4, 6) else j
+        return remote(src, dst, w_send.at[kind], w_recv.at[kind, slot], to)
+
+    def w_arrived(kind, j, n=3, slot=None):
+        ref = w1g.at[0 if kind < 3 else 1, pl.ds(0, n * wid), span[j]]
+        pltpu.make_async_copy(ref, ref, w_recv.at[kind, j if slot is None else slot]).wait()
 
     def w_sent(kind):
         ref = w1g.at[0, pl.ds(0, 3 * wid), :]
@@ -116,9 +117,8 @@
 
     for r in (PAIR, NEAR, DIAG):
         g_copy(r).start()
-    for i in range(2):
-        for r in (NEAR, DIAG):
-            in_copy(i, r).start()
+    for r in (NEAR, DIAG):
+        in_copy(0, r).start()
     for j in range(CHUNKS):
         for w in range(3):
             w_copy(3, w, j).start()
@@ -135,7 +135,11 @@
     def pass_cross(j):
         w_arrived(3, j)
         for w in range(3):
+            if j == 0 and w == 2:
+                for r in (NEAR, DIAG):
+                    in_copy(1, r).start()
             w_copy(4, w, j).start()
+        for w in range(3):
             w_copy(5, w, j).start()
 
     pass_cross(0)
@@ -169,16 +173,12 @@
         dy_t[:, rows] = dyg[rows, chip].astype(F32).T.astype(BF16)
         return carry
 
-    blocks(LN_ROWS, ln_rows)
-    for j in range(2, CHUNKS):
-        pass_cross(j)
-    for j in range(CHUNKS):
-        for w in range(3):
-            w_copy(0, w, j).start()
-    own_copy(1).wait()
-    for r in (PAIR, NEAR, DIAG):
-        in_copy(1, r).wait_recv()
-    blocks(LN_ROWS, dy_rows)
+    def early_act(k, rows, carry):
+        hr = h[rows, :]
+        u = dot(hr, w1g[1, :, span[0]])
+        v = dot(hr, w3g[1, :, span[0]])
+        act[rows, :size[0]] = (u * (1.0 / (1.0 + jnp.exp(-u))) * v).astype(BF16)
+        return carry
 
     def gated(s, j):
         n = size[j]
@@ -196,22 +196,32 @@
             return carry
         blocks(ROW_TILE, body)
 
-    def pair_copy(s, j):
-        return remote(part.at[s, 1 - c, :, span[j]], pair_in.at[s, :, span[j]], dw_send.at[s, j], dw_recv.at[s, j], dev[PAIR])
-
-    def weight_grads(s, j):
-        for k, (left, right) in enumerate(((h_t, du), (h_t, dv), (dy_t, act))):
+    EARLY, LATE = (2, 3, CHUNKS), (0, 2, 0)
+
+    def bands(j, piece):
+        lo, hi, slot = piece or (0, 3, j)
+        return pl.ds(lo * wid, (hi - lo) * wid), slot
+
+    def pair_copy(s, j, piece=None):
+        band, slot = bands(j, piece)
+        return remote(part.at[s, 1 - c, band, span[j]], pair_in.at[s, band, span[j]],
+                      dw_send.at[s, slot], dw_recv.at[s, slot], dev[PAIR])
+
+    def weight_grads(s, j, lo=0, hi=3):
+        for k, (left, right) in tuple(enumerate(((h_t, du), (h_t, dv), (dy_t, act))))[lo:hi]:
             full = dot(left[...], right[:, :size[j]])
             for b in range(2):
                 part[s, b, k * wid:(k + 1) * wid, span[j]] = full[b * wid:(b + 1) * wid, :]
 
-    def link_copy(j):
-        return remote(summed.at[:, span[j]], link_in.at[:, span[j]], lk_send.at[j], lk_recv.at[j], cross)
-
-    def send_sums(j):
-        pair_copy(1, j).wait_recv()
-        summed[:, span[j]] = part[1, c, :, span[j]] + pair_in[1, :, span[j]]
-        link_copy(j).start()
+    def link_copy(j, piece=None):
+        band, slot = bands(j, piece)
+        return remote(summed.at[band, span[j]], link_in.at[band, span[j]], lk_send.at[slot], lk_recv.at[slot], cross)
+
+    def send_sums(j, piece=None):
+        band, _ = bands(j, piece)
+        pair_copy(1, j, piece).wait_recv()
+        summed[band, span[j]] = part[1, c, band, span[j]] + pair_in[1, band, span[j]]
+        link_copy(j, piece).start()
 
     def token_sums(s, j, rows):
         n = size[j]
@@ -236,21 +246,47 @@
         for w in range(3):
             w_copy(6 if kind == 4 else 2, w, j).start()
 
-    pass_near(4, 0)
-    for j in range(CHUNKS):
-        w_arrived(5, j)
-        w_arrived(6, j)
+    blocks(LN_ROWS, ln_rows)
+    own_copy(1).wait()
+    in_copy(1, PAIR).wait_recv()
+    blocks(LN_ROWS, dy_rows)
+    pass_cross(2)
+    w_arrived(4, 0, 2)
+    for w in range(2):
+        w_copy(6, w, 0).start()
+    w_arrived(5, 0)
+    w_arrived(6, 0, 2)
+    blocks(ROW_TILE, early_act)
+    weight_grads(1, 0, 2, 3)
+    pair_copy(1, 0, EARLY).start()
+    for j in range(3, CHUNKS):
+        pass_cross(j)
+    for j in range(CHUNKS):
+        for w in range(3):
+            w_copy(0, w, j).start()
+    send_sums(0, EARLY)
+    for r in (NEAR, DIAG):
+        in_copy(1, r).wait_recv()
+
+    w_arrived(4, 0, 1, CHUNKS)
+    w_copy(6, 2, 0).start()
+    for j in range(CHUNKS):
+        if j:
+            w_arrived(5, j)
+            w_arrived(6, j)
+        else:
+            w_arrived(6, 0, 1, CHUNKS)
         if j > 1:
             send_sums(j - 1)
         gated(1, j)
-        weight_grads(1, j)
+        weight_grads(1, j, 0, 3 if j else 2)
         if j == 0:
-            pair_copy(1, j).start()
+            pair_copy(1, j, LATE).start()
         to_tokens(1, j, first=j == 0)
         if j:
             pair_copy(1, j).start()
         if j == 0:
-            send_sums(j)
+            send_sums(j, LATE)
         if j + 1 < CHUNKS:
             pass_near(4, j + 1)
         else:
@@ -258,7 +294,8 @@
 
     def finish_dw(j):
         pair_copy(0, j).wait_recv()
-        link_copy(j).wait_recv()
+        for piece in (EARLY, LATE) if j == 0 else (None,):
+            link_copy(j, piece).wait_recv()
         for k in range(3):
             band = pl.ds(k * wid, wid)
             total = part[0, c, band, span[j]] + pair_in[0, band, span[j]] + link_in[band, span[j]]
@@ -270,18 +307,14 @@
     lane = lax.broadcasted_iota(jnp.int32, (LN_ROWS, LN_ROWS), 1)
     last = CHUNKS - 1
 
-    def last_rows(k, rows, dg):
-        m, dh = token_sums(0, last, rows)
-        m_acc[rows, :] += m
-        dh = dh_acc[rows, :] + dh
-        dh_acc[rows, :] = dh
-        xh = xhat[rows, chip]
-        e = dh * gain_chip
+    def sum_rows(k, rows, carry):
+        e = dh_acc[rows, :] * gain_chip
         se = jnp.sum(e, axis=1, keepdims=True)
-        sex = jnp.sum(e * xh, axis=1, keepdims=True)
+        sex = jnp.sum(e * xhat[rows, chip], axis=1, keepdims=True)
         st_own[k] = jnp.where(lane == 0, se, jnp.where(lane == 1, sex, 0.0)).T[:8, :]
-        return dg + jnp.sum(dh * xh, axis=0, keepdims=True)
-
+        return carry
+
+    st_copy = remote(st_own, st_in, st_send, st_recv, dev[NEAR])
     for j in range(CHUNKS):
         w_arrived(1, j)
         w_arrived(2, j)
@@ -290,19 +323,18 @@
             ref = w1g.at[0, pl.ds(0, 3 * wid), :]
             pltpu.make_async_copy(ref, ref, lc_w).wait()
         gated(0, j)
+        weight_grads(0, j)
         if j < last:
-            weight_grads(0, j)
             to_tokens(0, j)
             pair_copy(0, j).start()
+            if j == last - 1:
+                blocks(LN_ROWS, sum_rows)
+                st_copy.start()
             pass_near(0, j + 1)
             if j:
                 finish_dw(j - 1)
-
-    dg = blocks(LN_ROWS, last_rows, jnp.zeros((1, half), F32))
-    st_copy = remote(st_own, st_in, st_send, st_recv, dev[NEAR])
-    st_copy.start()
-    weight_grads(0, last)
     pair_copy(0, last).start()
+    st_copy.wait_recv()
 
     outs, stage = (y_out, dx_out), (y_st, dx_st)
     mid = tok // 2
@@ -310,21 +342,37 @@
     def out_copy(i, part_of):
         rows = pl.ds(part_of * mid, mid)
         to_rows = pl.ds(pl.multiple_of(c * tok + part_of * mid, mid), mid)
-        src = y_st.at[rows, :] if i == 0 else dx_st.at[rows, core_cols(1 - c)]
-        return remote(src, outs[i].at[to_rows, :], out_send.at[i, part_of], out_recv.at[i, part_of], dev[PAIR])
+        return remote(stage[i].at[rows, core_cols(1 - c)], outs[i].at[to_rows, :],
+                      out_send.at[i, part_of], out_recv.at[i, part_of], dev[PAIR])
 
     def out_rows(k):
         return pl.ds(pl.multiple_of(c * tok + k * LN_ROWS, LN_ROWS), LN_ROWS)
 
-    def y_rows(k, rows, carry):
-        y_st[rows, :] = (xg[rows, col(PAIR)].astype(F32) + m_acc[rows, core_cols(1 - c)]).astype(BF16)
-        y_out[out_rows(k), :] = (xg[rows, col(OWN)].astype(F32) + m_acc[rows, core_cols(c)]).astype(BF16)
-        return carry
-
-    blocks(LN_ROWS, y_rows)
+    def last_rows(k, rows, dg):
+        n = size[last]
+        m = dot(act[rows, :n], w2g[0, span[last], chip])
+        full = dot_nt(du[rows, :n], w1g[0, :, span[last]]) + dot_nt(dv[rows, :n], w3g[0, :, span[last]])
+        dh_last[rows, :] = full
+        e = full * gain
+        before = jnp.concatenate([st_own[k] + st_in[k], jnp.zeros((LN_ROWS - 8, LN_ROWS), F32)], axis=0).T
+        me = (before[:, 0:1] + jnp.sum(e, axis=1, keepdims=True)) * (1.0 / d)
+        mex = (before[:, 1:2] + jnp.sum(e * xhat[rows, :], axis=1, keepdims=True)) * (1.0 / d)
+        dh = dh_acc[rows, :] + dh_last[rows, chip]
+        xh = xhat[rows, chip]
+        dx_ln = inv_std[rows, :] * (dh * gain_chip - me - xh * mex)
+        dx_st[rows, :] = (dyg[rows, chip].astype(F32) + dx_ln).astype(BF16)
+        dx_out[out_rows(k), :] = dx_st[rows, core_cols(c)]
+        y_st[rows, :] = (xg[rows, chip].astype(F32) + (m_acc[rows, :] + m)).astype(BF16)
+        y_out[out_rows(k), :] = y_st[rows, core_cols(c)]
+        return dg + jnp.sum(dh * xh, axis=0, keepdims=True)
+
+    dg = jnp.zeros((1, half), F32)
+    for b in range(2):
+        dg = blocks(LN_ROWS, last_rows, dg, lo=b * mid, hi=(b + 1) * mid)
+        out_copy(0, b).start()
+        out_copy(1, b).start()
     for b in range(2):
         dg_st[b] = dg[:, b * wid:(b + 1) * wid]
-        out_copy(0, b).start()
     dg_copies = [remote(dg_st.at[b], dg_in.at[k], dg_send.at[k], dg_recv.at[k], to)
                  for k, (b, to) in enumerate(((1 - c, dev[PAIR]), (c, cross), (1 - c, cross_pair)))]
     for cp in dg_copies:
@@ -336,25 +384,13 @@
             in_copy(i, r).wait_send()
     for kind in range(7):
         w_sent(kind)
-    for j in range(CHUNKS):
-        pair_copy(1, j).wait_send()
-        if j < last:
-            pair_copy(0, j).wait_send()
-        if j < last - 1:
-            link_copy(j).wait_send()
-    st_copy.wait_recv()
-
-    def dx_rows(k, rows, carry):
-        both = jnp.concatenate([st_own[k] + st_in[k], jnp.zeros((LN_ROWS - 8, LN_ROWS), F32)], axis=0).T * (1.0 / d)
-        e = dh_acc[rows, :] * gain_chip
-        dx_ln = inv_std[rows, :] * (e - both[:, 0:1] - xhat[rows, chip] * both[:, 1:2])
-        dx_st[rows, :] = (dyg[rows, chip].astype(F32) + dx_ln).astype(BF16)
-        dx_out[out_rows(k), :] = dx_st[rows, core_cols(c)]
-        return carry
-
-    for b in range(2):
-        blocks(LN_ROWS, dx_rows, lo=b * mid, hi=(b + 1) * mid)
-        out_copy(1, b).start()
+    st_copy.wait_send()
+    for j in range(CHUNKS):
+        pair_copy(0, j).wait_send()
+        for piece in (EARLY, LATE) if j == 0 else (None,):
+            pair_copy(1, j, piece).wait_send()
+            if j < last - 1:
+                link_copy(j, piece).wait_send()
 
     finish_dw(last - 1)
     finish_dw(last)
@@ -371,8 +407,6 @@
             out_copy(i, b).wait_recv()
     for cp in dg_copies:
         cp.wait_send()
-    st_copy.wait_send()
-    pair_copy(0, last).wait_send()
     link_copy(last - 1).wait_send()
     link_copy(last).wait_send()
 
@@ -408,12 +442,12 @@
                 vm((tok, d), BF16), vm((half, tok), BF16), vm((half, tok), BF16), vm((tok, d), F32), vm((tok, 1), F32),
                 vm((tok, fc), BF16), vm((tok, fc), BF16), vm((tok, fc), BF16),
                 vm((2, 2, 3 * wid, f), F32), vm((2, 3 * wid, f), F32), vm((3 * wid, f), F32), vm((3 * wid, f), F32),
-                vm((tok, half), F32), vm((tok, half), F32), vm((tok, wid), BF16), vm((tok, half), BF16),
+                vm((tok, half), F32), vm((tok, half), F32), vm((tok, d), F32), vm((tok, half), BF16), vm((tok, half), BF16),
                 vm((2, 1, wid), F32), vm((3, 1, wid), F32),
                 vm((tok // LN_ROWS, 8, LN_ROWS), F32), vm((tok // LN_ROWS, 8, LN_ROWS), F32),
                 dma((4,)), dma((4,)), dma((2, 4)), dma((2, 4)),
-                dma((7,)), dma((7, CHUNKS)), dma((2, CHUNKS)), dma((2, CHUNKS)),
-                dma((CHUNKS,)), dma((CHUNKS,)), dma((2, 2)), dma((2, 2)), dma((3,)), dma((3,)), dma(()), dma(()),
+                dma((7,)), dma((7, CHUNKS + 1)), dma((2, CHUNKS + 1)), dma((2, CHUNKS + 1)),
+                dma((CHUNKS + 1,)), dma((CHUNKS + 1,)), dma((2, 2)), dma((2, 2)), dma((3,)), dma((3,)), dma(()), dma(()),
                 dma((2,)), dma(()), dma(()),
             ],
             compiler_params=pltpu.CompilerParams(collective_id=0, has_side_effects=True,

time: 75.6 us -> 73.5 us (0.972)
  Pallas kernels: 74.7 us -> 72.6 us
    pallas_call x1, Pallas kernels: 73.2 us -> 71.1 us  [local_step(): pl.pallas_call(kernel, name='mlp_branch', out_shape=(jax.ShapeDtypeStruct...]
where the time goes in v5:
time: 73.5 us; the launch traced here: 73.4 us
  Pallas kernels  72.6 us (99%)
  between operations  0.8 us (1%)
    pallas_call x1, Pallas kernels, local_step(): pl.pallas_call(kernel, name='mlp_branch', out_shape=(jax.ShapeDtypeStruct...  71.1 us
    pallas_call x1, Pallas kernels, local_step(): pl.pallas_call(write_out, name='write_out', out_shape=tuple((jax.ShapeDty...  1.54 us

profile of v5, /device:TPU:0, one launch (start us, length us, event | category | flops | bytes accessed | tf_op | source)
XLA Modules:
  0.0 73.4 jit_solution(16605082290214931268)
XLA Ops:
  0.6 71.1 %mlp_branch.1 = (bf16[2048,128]{1,0:T(8,128)(2,1)S(1)}, bf16[2048,128]{1,0:T(8,128)(2,1)S(1)}, f32[128,1024]{1,0:T(8,128)S(1)}, f32[128,1024]{1,0:T(8,128)S(1)},...) custom-call(bf16[2048,128]{1,0:T(8,128)(2,1)} %x_in.1, bf16[2048,128]{1,0:T(8,128)(2,1)} %dy_in.1, f32[1,128]{1,0:T(1,128)} %bitcast.2, ...), custom_call_target="tpu_custom_call" | custom-call | tf_op jit(solution)/shard_map/mlp_branch/pallas_call | solution.py:431
  71.7 1.5 %write_out.1 = (bf16[2048,128]{1,0:T(8,128)(2,1)}, bf16[2048,128]{1,0:T(8,128)(2,1)}, f32[128,1024]{1,0:T(8,128)}, f32[128,1024]{1,0:T(8,128)}, f32[1024,128]{1,0:T(8,128)}, /*index=5*/f32[1,128]{1,0:T(1,128)}) custom-call(bf16[2048,128]{1,0:T(8,128)(2,1)S(1)} %get-tuple-element.18.refs_0_, bf16[2048,128]{1,0:T(8,128)(2,1)S(1)} %get-tuple-element.19.refs_1_, ...), custom_call_target="tpu_custom_call" | custom-call | tf_op jit(solution)/shard_map/write_out/pallas_call | solution.py:456

commit v6 on v5

--- a/solution.py
+++ b/solution.py
@@ -27,8 +27,8 @@
 
 def kernel(x_in, dy_in, g_in, w1_in, w3_in, w2_in,
            y_out, dx_out, dw1_out, dw3_out, dw2_out, dg_out,
-           xg, dyg, gg, w1g, w3g, w2g, h, h_t, dy_t, xhat, inv_std, act, du, dv, part, pair_in, summed, link_in,
-           m_acc, dh_acc, dh_last, y_st, dx_st, dg_st, dg_in, st_own, st_in,
+           xg, dyg, gg, w1g, w3g, w2g, h, h_t, dy_t, xhat, inv_std, uv, act, du, dv, part, pair_in, summed, link_in,
+           m_acc, dh_acc, dh_last, means, y_st, dx_st, dg_st, dg_in, st_own, st_in,
            g_send, g_recv, in_send, in_recv, w_send, w_recv, dw_send, dw_recv,
            lk_send, lk_recv, out_send, out_recv, dg_send, dg_recv, st_send, st_recv, lc_in, lc_w, lc_g):
     y, t = lax.axis_index("ty"), lax.axis_index("tx")
@@ -68,13 +68,13 @@
     tin, tg = (x_in, dy_in), (xg, dyg)
 
     def in_copy(i, r):
-        return remote(tin[i].at[rows_of(peer_c[r]), :], tg[i].at[:, col(OWN)], in_send.at[i, r], in_recv.at[i, r], dev[r])
+        return remote(tin[i].at[rows_of(peer_c[r]), :], tg[i].at[:, col(OWN)], in_send, in_recv.at[i, r - 1], dev[r])
 
     def own_copy(i):
         return pltpu.make_async_copy(tin[i].at[rows_of(c), :], tg[i].at[:, col(OWN)], lc_in.at[i])
 
     def g_copy(r):
-        return remote(g_in, gg.at[t], g_send.at[r], g_recv.at[r], dev[r])
+        return remote(g_in, gg.at[t], g_send, g_recv, dev[r])
 
     def w_src(w, j):
         if w == 2:
@@ -101,16 +101,13 @@
             src, dst, to = w_dst(w, 1, j, OWN), w_dst(w, 1, j, OWN), dev[PAIR]
         else:
             src, dst, to = w_dst(w, 1, j, NEAR), w_dst(w, 1, j, NEAR), dev[PAIR]
-        slot = CHUNKS if w == 2 and j == 0 and kind in (4, 6) else j
-        return remote(src, dst, w_send.at[kind], w_recv.at[kind, slot], to)
-
-    def w_arrived(kind, j, n=3, slot=None):
-        ref = w1g.at[0 if kind < 3 else 1, pl.ds(0, n * wid), span[j]]
-        pltpu.make_async_copy(ref, ref, w_recv.at[kind, j if slot is None else slot]).wait()
-
-    def w_sent(kind):
-        ref = w1g.at[0, pl.ds(0, 3 * wid), :]
-        pltpu.make_async_copy(ref, ref, w_send.at[kind]).wait()
+        return remote(src, dst, w_send.at[kind // 4], w_recv.at[kind, j], to)
+
+    def all_of(ref, sem):
+        pltpu.make_async_copy(ref, ref, sem).wait()
+
+    def w_arrived(kind, j):
+        all_of(w1g.at[0 if kind < 3 else 1, pl.ds(0, 3 * wid), span[j]], w_recv.at[kind, j])
 
     def own_w(w, j):
         return pltpu.make_async_copy(w_src(w, j), w_dst(w, 0, j, OWN), lc_w)
@@ -135,10 +132,10 @@
     def pass_cross(j):
         w_arrived(3, j)
         for w in range(3):
-            if j == 0 and w == 2:
-                for r in (NEAR, DIAG):
-                    in_copy(1, r).start()
             w_copy(4, w, j).start()
+        if j == 0:
+            for r in (NEAR, DIAG):
+                in_copy(1, r).start()
         for w in range(3):
             w_copy(5, w, j).start()
 
@@ -148,7 +145,7 @@
     own_g.wait()
     for r in (PAIR, NEAR, DIAG):
         in_copy(0, r).wait_recv()
-        g_copy(r).wait_recv()
+    all_of(gg.at[pl.ds(0, 3)], g_recv)
     gain = jnp.concatenate([gg[k] for k in range(4)], axis=1)
     gain_chip = jnp.concatenate([gg[2 * x], gg[2 * x + 1]], axis=1)
 
@@ -177,26 +174,33 @@
         hr = h[rows, :]
         u = dot(hr, w1g[1, :, span[0]])
         v = dot(hr, w3g[1, :, span[0]])
+        uv[0, rows, :] = u
+        uv[1, rows, :] = v
         act[rows, :size[0]] = (u * (1.0 / (1.0 + jnp.exp(-u))) * v).astype(BF16)
         return carry
 
-    def gated(s, j):
+    def gated(s, j, known=False):
         n = size[j]
 
         def body(k, rows, carry):
-            hr = h[rows, :]
-            u = dot(hr, w1g[s, :, span[j]])
-            v = dot(hr, w3g[s, :, span[j]])
+            if known:
+                u, v = uv[0, rows, :], uv[1, rows, :]
+            else:
+                hr = h[rows, :]
+                u = dot(hr, w1g[s, :, span[j]])
+                v = dot(hr, w3g[s, :, span[j]])
             da = dot_nt(dyg[rows, :], w2g[s, span[j], :])
             sig = 1.0 / (1.0 + jnp.exp(-u))
             swish = u * sig
-            act[rows, :n] = (swish * v).astype(BF16)
+            if not known:
+                act[rows, :n] = (swish * v).astype(BF16)
             du[rows, :n] = (da * v * sig * (1.0 + u * (1.0 - sig))).astype(BF16)
             dv[rows, :n] = (da * swish).astype(BF16)
             return carry
         blocks(ROW_TILE, body)
 
-    EARLY, LATE = (2, 3, CHUNKS), (0, 2, 0)
+    EARLY, LATE1, LATE3 = (2, 3, CHUNKS), (0, 1, 0), (1, 2, CHUNKS + 1)
+    FIRST = (EARLY, LATE1, LATE3)
 
     def bands(j, piece):
         lo, hi, slot = piece or (0, 3, j)
@@ -205,7 +209,7 @@
     def pair_copy(s, j, piece=None):
         band, slot = bands(j, piece)
         return remote(part.at[s, 1 - c, band, span[j]], pair_in.at[s, band, span[j]],
-                      dw_send.at[s, slot], dw_recv.at[s, slot], dev[PAIR])
+                      dw_send, dw_recv.at[s, slot], dev[PAIR])
 
     def weight_grads(s, j, lo=0, hi=3):
         for k, (left, right) in tuple(enumerate(((h_t, du), (h_t, dv), (dy_t, act))))[lo:hi]:
@@ -215,7 +219,7 @@
 
     def link_copy(j, piece=None):
         band, slot = bands(j, piece)
-        return remote(summed.at[band, span[j]], link_in.at[band, span[j]], lk_send.at[slot], lk_recv.at[slot], cross)
+        return remote(summed.at[band, span[j]], link_in.at[band, span[j]], lk_send, lk_recv.at[slot], cross)
 
     def send_sums(j, piece=None):
         band, _ = bands(j, piece)
@@ -251,11 +255,9 @@
     in_copy(1, PAIR).wait_recv()
     blocks(LN_ROWS, dy_rows)
     pass_cross(2)
-    w_arrived(4, 0, 2)
-    for w in range(2):
-        w_copy(6, w, 0).start()
+    pass_near(4, 0)
     w_arrived(5, 0)
-    w_arrived(6, 0, 2)
+    w_arrived(6, 0)
     blocks(ROW_TILE, early_act)
     weight_grads(1, 0, 2, 3)
     pair_copy(1, 0, EARLY).start()
@@ -268,25 +270,25 @@
     for r in (NEAR, DIAG):
         in_copy(1, r).wait_recv()
 
-    w_arrived(4, 0, 1, CHUNKS)
-    w_copy(6, 2, 0).start()
     for j in range(CHUNKS):
         if j:
             w_arrived(5, j)
             w_arrived(6, j)
-        else:
-            w_arrived(6, 0, 1, CHUNKS)
         if j > 1:
             send_sums(j - 1)
-        gated(1, j)
-        weight_grads(1, j, 0, 3 if j else 2)
+        gated(1, j, known=j == 0)
         if j == 0:
-            pair_copy(1, j, LATE).start()
+            for k, piece in enumerate((LATE1, LATE3)):
+                weight_grads(1, j, k, k + 1)
+                pair_copy(1, j, piece).start()
+        else:
+            weight_grads(1, j)
         to_tokens(1, j, first=j == 0)
-        if j:
+        if j == 0:
+            send_sums(j, LATE1)
+            send_sums(j, LATE3)
+        else:
             pair_copy(1, j).start()
-        if j == 0:
-            send_sums(j, LATE)
         if j + 1 < CHUNKS:
             pass_near(4, j + 1)
         else:
@@ -294,7 +296,7 @@
 
     def finish_dw(j):
         pair_copy(0, j).wait_recv()
-        for piece in (EARLY, LATE) if j == 0 else (None,):
+        for piece in FIRST if j == 0 else (None,):
             link_copy(j, piece).wait_recv()
         for k in range(3):
             band = pl.ds(k * wid, wid)
@@ -343,72 +345,56 @@
         rows = pl.ds(part_of * mid, mid)
         to_rows = pl.ds(pl.multiple_of(c * tok + part_of * mid, mid), mid)
         return remote(stage[i].at[rows, core_cols(1 - c)], outs[i].at[to_rows, :],
-                      out_send.at[i, part_of], out_recv.at[i, part_of], dev[PAIR])
+                      out_send, out_recv, dev[PAIR])
 
     def out_rows(k):
         return pl.ds(pl.multiple_of(c * tok + k * LN_ROWS, LN_ROWS), LN_ROWS)
 
     def last_rows(k, rows, dg):
         n = size[last]
-        m = dot(act[rows, :n], w2g[0, span[last], chip])
         full = dot_nt(du[rows, :n], w1g[0, :, span[last]]) + dot_nt(dv[rows, :n], w3g[0, :, span[last]])
         dh_last[rows, :] = full
         e = full * gain
         before = jnp.concatenate([st_own[k] + st_in[k], jnp.zeros((LN_ROWS - 8, LN_ROWS), F32)], axis=0).T
-        me = (before[:, 0:1] + jnp.sum(e, axis=1, keepdims=True)) * (1.0 / d)
-        mex = (before[:, 1:2] + jnp.sum(e * xhat[rows, :], axis=1, keepdims=True)) * (1.0 / d)
+        means[0, rows, :] = (before[:, 0:1] + jnp.sum(e, axis=1, keepdims=True)) * (1.0 / d)
+        means[1, rows, :] = (before[:, 1:2] + jnp.sum(e * xhat[rows, :], axis=1, keepdims=True)) * (1.0 / d)
         dh = dh_acc[rows, :] + dh_last[rows, chip]
-        xh = xhat[rows, chip]
-        dx_ln = inv_std[rows, :] * (dh * gain_chip - me - xh * mex)
+        dh_acc[rows, :] = dh
+        return dg + jnp.sum(dh * xhat[rows, chip], axis=0, keepdims=True)
+
+    def out_blocks(k, rows, carry):
+        dx_ln = inv_std[rows, :] * (dh_acc[rows, :] * gain_chip - means[0, rows, :] - xhat[rows, chip] * means[1, rows, :])
         dx_st[rows, :] = (dyg[rows, chip].astype(F32) + dx_ln).astype(BF16)
         dx_out[out_rows(k), :] = dx_st[rows, core_cols(c)]
+        m = dot(act[rows, :size[last]], w2g[0, span[last], chip])
         y_st[rows, :] = (xg[rows, chip].astype(F32) + (m_acc[rows, :] + m)).astype(BF16)
         y_out[out_rows(k), :] = y_st[rows, core_cols(c)]
-        return dg + jnp.sum(dh * xh, axis=0, keepdims=True)
-
-    dg = jnp.zeros((1, half), F32)
+        return carry
+
+    dg = blocks(LN_ROWS, last_rows, jnp.zeros((1, half), F32))
     for b in range(2):
-        dg = blocks(LN_ROWS, last_rows, dg, lo=b * mid, hi=(b + 1) * mid)
+        dg_st[b] = dg[:, b * wid:(b + 1) * wid]
+    for k, (b, to) in enumerate(((1 - c, dev[PAIR]), (c, cross), (1 - c, cross_pair))):
+        remote(dg_st.at[b], dg_in.at[k], dg_send, dg_recv, to).start()
+    for b in range(2):
+        blocks(LN_ROWS, out_blocks, lo=b * mid, hi=(b + 1) * mid)
         out_copy(0, b).start()
         out_copy(1, b).start()
-    for b in range(2):
-        dg_st[b] = dg[:, b * wid:(b + 1) * wid]
-    dg_copies = [remote(dg_st.at[b], dg_in.at[k], dg_send.at[k], dg_recv.at[k], to)
-                 for k, (b, to) in enumerate(((1 - c, dev[PAIR]), (c, cross), (1 - c, cross_pair)))]
-    for cp in dg_copies:
-        cp.start()
-
-    for r in (PAIR, NEAR, DIAG):
-        g_copy(r).wait_send()
-        for i in range(2):
-            in_copy(i, r).wait_send()
-    for kind in range(7):
-        w_sent(kind)
+
+    all_of(gg.at[pl.ds(0, 3)], g_send)
+    all_of(part.at[0, 0], in_send)
+    all_of(part.at[0], w_send.at[0])
+    all_of(part.at[0, :, :, pl.ds(0, 6 * unit)], w_send.at[1])
+    all_of(part.at[0], dw_send)
     st_copy.wait_send()
-    for j in range(CHUNKS):
-        pair_copy(0, j).wait_send()
-        for piece in (EARLY, LATE) if j == 0 else (None,):
-            pair_copy(1, j, piece).wait_send()
-            if j < last - 1:
-                link_copy(j, piece).wait_send()
-
     finish_dw(last - 1)
     finish_dw(last)
-
-    total_dg = dg_st[c]
-    for k, cp in enumerate(dg_copies):
-        cp.wait_recv()
-        total_dg = total_dg + dg_in[k]
-    dg_out[...] = total_dg
-
-    for i in range(2):
-        for b in range(2):
-            out_copy(i, b).wait_send()
-            out_copy(i, b).wait_recv()
-    for cp in dg_copies:
-        cp.wait_send()
-    link_copy(last - 1).wait_send()
-    link_copy(last).wait_send()
+    all_of(dg_in, dg_recv)
+    dg_out[...] = dg_st[c] + dg_in[0] + dg_in[1] + dg_in[2]
+    all_of(dg_in, dg_send)
+    all_of(part.at[0, 0], lk_send)
+    all_of(dyg.at[pl.ds(0, mid), :], out_send)
+    all_of(dyg.at[pl.ds(0, mid), :], out_recv)
 
 
 def write_out(*refs):
@@ -440,14 +426,16 @@
                 vm((tok, d), BF16), vm((tok, d), BF16), vm((4, 1, wid), F32),
                 vm((2, d, f), BF16), vm((2, d, f), BF16), vm((2, f, d), BF16),
                 vm((tok, d), BF16), vm((half, tok), BF16), vm((half, tok), BF16), vm((tok, d), F32), vm((tok, 1), F32),
+                vm((2, tok, f // 8 * EIGHTHS[0]), F32),
                 vm((tok, fc), BF16), vm((tok, fc), BF16), vm((tok, fc), BF16),
                 vm((2, 2, 3 * wid, f), F32), vm((2, 3 * wid, f), F32), vm((3 * wid, f), F32), vm((3 * wid, f), F32),
-                vm((tok, half), F32), vm((tok, half), F32), vm((tok, d), F32), vm((tok, half), BF16), vm((tok, half), BF16),
+                vm((tok, half), F32), vm((tok, half), F32), vm((tok, d), F32), vm((2, tok, 1), F32),
+                vm((tok, half), BF16), vm((tok, half), BF16),
                 vm((2, 1, wid), F32), vm((3, 1, wid), F32),
                 vm((tok // LN_ROWS, 8, LN_ROWS), F32), vm((tok // LN_ROWS, 8, LN_ROWS), F32),
-                dma((4,)), dma((4,)), dma((2, 4)), dma((2, 4)),
-                dma((7,)), dma((7, CHUNKS + 1)), dma((2, CHUNKS + 1)), dma((2, CHUNKS + 1)),
-                dma((CHUNKS + 1,)), dma((CHUNKS + 1,)), dma((2, 2)), dma((2, 2)), dma((3,)), dma((3,)), dma(()), dma(()),
+                dma(()), dma(()), dma(()), dma((2, 3)),
+                dma((2,)), dma((7, CHUNKS)), dma(()), dma((2, CHUNKS + 2)),
+                dma(()), dma((CHUNKS + 2,)), dma(()), dma(()), dma(()), dma(()), dma(()), dma(()),
                 dma((2,)), dma(()), dma(()),
             ],
             compiler_params=pltpu.CompilerParams(collective_id=0, has_side_effects=True,

time: 73.5 us -> 72.9 us (level)
  no operation moved by 1% of the time
where the time goes in v6:
time: 72.9 us; the launch traced here: 72.8 us
  Pallas kernels  72 us (99%)
  between operations  0.8 us (1%)
    pallas_call x1, Pallas kernels, local_step(): pl.pallas_call(kernel, name='mlp_branch', out_shape=(jax.ShapeDtypeStruct...  70.5 us
    pallas_call x1, Pallas kernels, local_step(): pl.pallas_call(write_out, name='write_out', out_shape=tuple((jax.ShapeDty...  1.54 us

profile of v6, /device:TPU:0, one launch (start us, length us, event | category | flops | bytes accessed | tf_op | source)
XLA Modules:
  0.0 72.8 jit_solution(16523014116038265497)
XLA Ops:
  0.6 70.5 %mlp_branch.1 = (bf16[2048,128]{1,0:T(8,128)(2,1)S(1)}, bf16[2048,128]{1,0:T(8,128)(2,1)S(1)}, f32[128,1024]{1,0:T(8,128)S(1)}, f32[128,1024]{1,0:T(8,128)S(1)},...) custom-call(bf16[2048,128]{1,0:T(8,128)(2,1)} %x_in.1, bf16[2048,128]{1,0:T(8,128)(2,1)} %dy_in.1, f32[1,128]{1,0:T(1,128)} %bitcast.2, ...), custom_call_target="tpu_custom_call" | custom-call | tf_op jit(solution)/shard_map/mlp_branch/pallas_call | solution.py:417
  71.1 1.5 %write_out.1 = (bf16[2048,128]{1,0:T(8,128)(2,1)}, bf16[2048,128]{1,0:T(8,128)(2,1)}, f32[128,1024]{1,0:T(8,128)}, f32[128,1024]{1,0:T(8,128)}, f32[1024,128]{1,0:T(8,128)}, /*index=5*/f32[1,128]{1,0:T(1,128)}) custom-call(bf16[2048,128]{1,0:T(8,128)(2,1)S(1)} %get-tuple-element.18.refs_0_, bf16[2048,128]{1,0:T(8,128)(2,1)S(1)} %get-tuple-element.19.refs_1_, ...), custom_call_target="tpu_custom_call" | custom-call | tf_op jit(solution)/shard_map/write_out/pallas_call | solution.py:444

commit v7 on v6

--- a/solution.py
+++ b/solution.py
@@ -28,7 +28,7 @@
 def kernel(x_in, dy_in, g_in, w1_in, w3_in, w2_in,
            y_out, dx_out, dw1_out, dw3_out, dw2_out, dg_out,
            xg, dyg, gg, w1g, w3g, w2g, h, h_t, dy_t, xhat, inv_std, uv, act, du, dv, part, pair_in, summed, link_in,
-           m_acc, dh_acc, dh_last, means, y_st, dx_st, dg_st, dg_in, st_own, st_in,
+           m_acc, dh_acc, dh_last, y_st, dx_st, dg_st, dg_in, st_own, st_in,
            g_send, g_recv, in_send, in_recv, w_send, w_recv, dw_send, dw_recv,
            lk_send, lk_recv, out_send, out_recv, dg_send, dg_recv, st_send, st_recv, lc_in, lc_w, lc_g):
     y, t = lax.axis_index("ty"), lax.axis_index("tx")
@@ -101,13 +101,14 @@
             src, dst, to = w_dst(w, 1, j, OWN), w_dst(w, 1, j, OWN), dev[PAIR]
         else:
             src, dst, to = w_dst(w, 1, j, NEAR), w_dst(w, 1, j, NEAR), dev[PAIR]
-        return remote(src, dst, w_send.at[kind // 4], w_recv.at[kind, j], to)
+        slot = CHUNKS if kind in (0, 2) and w == 2 and j == CHUNKS - 1 else j
+        return remote(src, dst, w_send.at[kind // 4], w_recv.at[kind, slot], to)
 
     def all_of(ref, sem):
         pltpu.make_async_copy(ref, ref, sem).wait()
 
-    def w_arrived(kind, j):
-        all_of(w1g.at[0 if kind < 3 else 1, pl.ds(0, 3 * wid), span[j]], w_recv.at[kind, j])
+    def w_arrived(kind, j, n=3, slot=None):
+        all_of(w1g.at[0 if kind < 3 else 1, pl.ds(0, n * wid), span[j]], w_recv.at[kind, j if slot is None else slot])
 
     def own_w(w, j):
         return pltpu.make_async_copy(w_src(w, j), w_dst(w, 0, j, OWN), lc_w)
@@ -170,14 +171,16 @@
         dy_t[:, rows] = dyg[rows, chip].astype(F32).T.astype(BF16)
         return carry
 
-    def early_act(k, rows, carry):
-        hr = h[rows, :]
-        u = dot(hr, w1g[1, :, span[0]])
-        v = dot(hr, w3g[1, :, span[0]])
-        uv[0, rows, :] = u
-        uv[1, rows, :] = v
-        act[rows, :size[0]] = (u * (1.0 / (1.0 + jnp.exp(-u))) * v).astype(BF16)
-        return carry
+    def early_act(s, j):
+        def body(k, rows, carry):
+            hr = h[rows, :]
+            u = dot(hr, w1g[s, :, span[j]])
+            v = dot(hr, w3g[s, :, span[j]])
+            uv[0, rows, :] = u
+            uv[1, rows, :] = v
+            act[rows, :size[j]] = (u * (1.0 / (1.0 + jnp.exp(-u))) * v).astype(BF16)
+            return carry
+        blocks(ROW_TILE, body)
 
     def gated(s, j, known=False):
         n = size[j]
@@ -246,8 +249,9 @@
         blocks(ROW_TILE, body)
 
     def pass_near(kind, j):
-        w_arrived(kind, j)
-        for w in range(3):
+        n = 2 if kind == 0 and j == CHUNKS - 1 else 3
+        w_arrived(kind, j, n)
+        for w in range(n):
             w_copy(6 if kind == 4 else 2, w, j).start()
 
     blocks(LN_ROWS, ln_rows)
@@ -258,7 +262,7 @@
     pass_near(4, 0)
     w_arrived(5, 0)
     w_arrived(6, 0)
-    blocks(ROW_TILE, early_act)
+    early_act(1, 0)
     weight_grads(1, 0, 2, 3)
     pair_copy(1, 0, EARLY).start()
     for j in range(3, CHUNKS):
@@ -274,7 +278,7 @@
         if j:
             w_arrived(5, j)
             w_arrived(6, j)
-        if j > 1:
+        if j > 2:
             send_sums(j - 1)
         gated(1, j, known=j == 0)
         if j == 0:
@@ -283,16 +287,20 @@
                 pair_copy(1, j, piece).start()
         else:
             weight_grads(1, j)
+        if j == 1:
+            pair_copy(1, j).start()
+        if j + 1 == CHUNKS:
+            pass_near(0, 0)
         to_tokens(1, j, first=j == 0)
         if j == 0:
             send_sums(j, LATE1)
             send_sums(j, LATE3)
+        elif j == 1:
+            send_sums(j)
         else:
             pair_copy(1, j).start()
         if j + 1 < CHUNKS:
             pass_near(4, j + 1)
-        else:
-            pass_near(0, 0)
 
     def finish_dw(j):
         pair_copy(0, j).wait_recv()
@@ -319,24 +327,32 @@
     st_copy = remote(st_own, st_in, st_send, st_recv, dev[NEAR])
     for j in range(CHUNKS):
         w_arrived(1, j)
-        w_arrived(2, j)
+        w_arrived(2, j, 2 if j == last else 3)
         if j == 0:
             send_sums(last)
             ref = w1g.at[0, pl.ds(0, 3 * wid), :]
             pltpu.make_async_copy(ref, ref, lc_w).wait()
-        gated(0, j)
-        weight_grads(0, j)
+        if j == last:
+            early_act(0, j)
+            weight_grads(0, j, 2, 3)
+            w_arrived(2, j, 1, CHUNKS)
+        gated(0, j, known=j == last)
+        weight_grads(0, j, 0, 2 if j == last else 3)
         if j < last:
+            if j != last - 2:
+                pass_near(0, j + 1)
             to_tokens(0, j)
             pair_copy(0, j).start()
+            if j == last - 2:
+                pass_near(0, j + 1)
             if j == last - 1:
                 blocks(LN_ROWS, sum_rows)
                 st_copy.start()
-            pass_near(0, j + 1)
+                w_arrived(0, last, 1, CHUNKS)
+                w_copy(2, 2, last).start()
             if j:
                 finish_dw(j - 1)
     pair_copy(0, last).start()
-    st_copy.wait_recv()
 
     outs, stage = (y_out, dx_out), (y_st, dx_st)
     mid = tok // 2
@@ -352,18 +368,17 @@
 
     def last_rows(k, rows, dg):
         n = size[last]
-        full = dot_nt(du[rows, :n], w1g[0, :, span[last]]) + dot_nt(dv[rows, :n], w3g[0, :, span[last]])
-        dh_last[rows, :] = full
-        e = full * gain
-        before = jnp.concatenate([st_own[k] + st_in[k], jnp.zeros((LN_ROWS - 8, LN_ROWS), F32)], axis=0).T
-        means[0, rows, :] = (before[:, 0:1] + jnp.sum(e, axis=1, keepdims=True)) * (1.0 / d)
-        means[1, rows, :] = (before[:, 1:2] + jnp.sum(e * xhat[rows, :], axis=1, keepdims=True)) * (1.0 / d)
+        dh_last[rows, :] = dot_nt(du[rows, :n], w1g[0, :, span[last]]) + dot_nt(dv[rows, :n], w3g[0, :, span[last]])
         dh = dh_acc[rows, :] + dh_last[rows, chip]
         dh_acc[rows, :] = dh
         return dg + jnp.sum(dh * xhat[rows, chip], axis=0, keepdims=True)
 
     def out_blocks(k, rows, carry):
-        dx_ln = inv_std[rows, :] * (dh_acc[rows, :] * gain_chip - means[0, rows, :] - xhat[rows, chip] * means[1, rows, :])
+        e = dh_last[rows, :] * gain
+        before = jnp.concatenate([st_own[k] + st_in[k], jnp.zeros((LN_ROWS - 8, LN_ROWS), F32)], axis=0).T
+        me = (before[:, 0:1] + jnp.sum(e, axis=1, keepdims=True)) * (1.0 / d)
+        mex = (before[:, 1:2] + jnp.sum(e * xhat[rows, :], axis=1, keepdims=True)) * (1.0 / d)
+        dx_ln = inv_std[rows, :] * (dh_acc[rows, :] * gain_chip - me - xhat[rows, chip] * mex)
         dx_st[rows, :] = (dyg[rows, chip].astype(F32) + dx_ln).astype(BF16)
         dx_out[out_rows(k), :] = dx_st[rows, core_cols(c)]
         m = dot(act[rows, :size[last]], w2g[0, span[last], chip])
@@ -376,6 +391,7 @@
         dg_st[b] = dg[:, b * wid:(b + 1) * wid]
     for k, (b, to) in enumerate(((1 - c, dev[PAIR]), (c, cross), (1 - c, cross_pair))):
         remote(dg_st.at[b], dg_in.at[k], dg_send, dg_recv, to).start()
+    st_copy.wait_recv()
     for b in range(2):
         blocks(LN_ROWS, out_blocks, lo=b * mid, hi=(b + 1) * mid)
         out_copy(0, b).start()
@@ -429,12 +445,12 @@
                 vm((2, tok, f // 8 * EIGHTHS[0]), F32),
                 vm((tok, fc), BF16), vm((tok, fc), BF16), vm((tok, fc), BF16),
                 vm((2, 2, 3 * wid, f), F32), vm((2, 3 * wid, f), F32), vm((3 * wid, f), F32), vm((3 * wid, f), F32),
-                vm((tok, half), F32), vm((tok, half), F32), vm((tok, d), F32), vm((2, tok, 1), F32),
+                vm((tok, half), F32), vm((tok, half), F32), vm((tok, d), F32),
                 vm((tok, half), BF16), vm((tok, half), BF16),
                 vm((2, 1, wid), F32), vm((3, 1, wid), F32),
                 vm((tok // LN_ROWS, 8, LN_ROWS), F32), vm((tok // LN_ROWS, 8, LN_ROWS), F32),
                 dma(()), dma(()), dma(()), dma((2, 3)),
-                dma((2,)), dma((7, CHUNKS)), dma(()), dma((2, CHUNKS + 2)),
+                dma((2,)), dma((7, CHUNKS + 1)), dma(()), dma((2, CHUNKS + 2)),
                 dma(()), dma((CHUNKS + 2,)), dma(()), dma(()), dma(()), dma(()), dma(()), dma(()),
                 dma((2,)), dma(()), dma(()),
             ],

time: 72.9 us -> 72.3 us (level)
  no operation moved by 1% of the time
where the time goes in v7:
time: 72.3 us; the launch traced here: 72.2 us
  Pallas kernels  71.4 us (99%)
  between operations  0.8 us (1%)
    pallas_call x1, Pallas kernels, local_step(): pl.pallas_call(kernel, name='mlp_branch', out_shape=(jax.ShapeDtypeStruct...  69.9 us
    pallas_call x1, Pallas kernels, local_step(): pl.pallas_call(write_out, name='write_out', out_shape=tuple((jax.ShapeDty...  1.54 us

profile of v7, /device:TPU:0, one launch (start us, length us, event | category | flops | bytes accessed | tf_op | source)
XLA Modules:
  0.0 72.2 jit_solution(6240203700471043404)
XLA Ops:
  0.6 69.9 %mlp_branch.1 = (bf16[2048,128]{1,0:T(8,128)(2,1)S(1)}, bf16[2048,128]{1,0:T(8,128)(2,1)S(1)}, f32[128,1024]{1,0:T(8,128)S(1)}, f32[128,1024]{1,0:T(8,128)S(1)},...) custom-call(bf16[2048,128]{1,0:T(8,128)(2,1)} %x_in.1, bf16[2048,128]{1,0:T(8,128)(2,1)} %dy_in.1, f32[1,128]{1,0:T(1,128)} %bitcast.2, ...), custom_call_target="tpu_custom_call" | custom-call | tf_op jit(solution)/shard_map/mlp_branch/pallas_call | solution.py:433
  70.5 1.5 %write_out.1 = (bf16[2048,128]{1,0:T(8,128)(2,1)}, bf16[2048,128]{1,0:T(8,128)(2,1)}, f32[128,1024]{1,0:T(8,128)}, f32[128,1024]{1,0:T(8,128)}, f32[1024,128]{1,0:T(8,128)}, /*index=5*/f32[1,128]{1,0:T(1,128)}) custom-call(bf16[2048,128]{1,0:T(8,128)(2,1)S(1)} %get-tuple-element.18.refs_0_, bf16[2048,128]{1,0:T(8,128)(2,1)S(1)} %get-tuple-element.19.refs_1_, ...), custom_call_target="tpu_custom_call" | custom-call | tf_op jit(solution)/shard_map/write_out/pallas_call | solution.py:460

commit v8 on v7

--- a/solution.py
+++ b/solution.py
@@ -15,6 +15,7 @@
 CHUNKS = len(EIGHTHS)
 LN_ROWS = 128
 ROW_TILE = 256
+PIECES = 4
 
 
 def dot(a, b):
@@ -415,7 +416,13 @@
 
 def write_out(*refs):
     n = len(refs) // 2
-    copies = [pltpu.make_async_copy(refs[i], refs[n + i], refs[2 * n].at[i]) for i in range(n)]
+    copies = []
+    for i in range(n):
+        rows = refs[i].shape[0]
+        pieces = PIECES if rows > PIECES else 1
+        for k in range(pieces):
+            at = pl.ds(k * (rows // pieces), rows // pieces)
+            copies.append(pltpu.make_async_copy(refs[i].at[at, :], refs[n + i].at[at, :], refs[2 * n].at[i, k]))
     for cp in copies:
         cp.start()
     for cp in copies:
@@ -463,7 +470,7 @@
             out_shape=tuple(jax.ShapeDtypeStruct(o.shape, o.dtype) for o in outs),
             in_specs=[in_vmem] * 6,
             out_specs=(pl.BlockSpec(memory_space=pl.ANY),) * 6,
-            scratch_shapes=[dma((6,))],
+            scratch_shapes=[dma((6, PIECES))],
             compiler_params=pltpu.CompilerParams(vmem_limit_bytes=2 ** 20),
         )(*outs)
         return outs[:5] + (outs[5].reshape(wid),)

time: 72.3 us -> 72.4 us (level)
  no operation moved by 1% of the time
where the time goes in v8:
time: 72.4 us; the launch traced here: 72.3 us
  Pallas kernels  71.5 us (99%)
  between operations  0.8 us (1%)
    pallas_call x1, Pallas kernels, local_step(): pl.pallas_call(kernel, name='mlp_branch', out_shape=(jax.ShapeDtypeStruct...  69.9 us
    pallas_call x1, Pallas kernels, local_step(): pl.pallas_call(write_out, name='write_out', out_shape=tuple((jax.ShapeDty...  1.69 us

profile of v8, /device:TPU:0, one launch (start us, length us, event | category | flops | bytes accessed | tf_op | source)
XLA Modules:
  0.0 72.3 jit_solution(4880580619490099051)
XLA Ops:
  0.6 69.9 %mlp_branch.1 = (bf16[2048,128]{1,0:T(8,128)(2,1)S(1)}, bf16[2048,128]{1,0:T(8,128)(2,1)S(1)}, f32[128,1024]{1,0:T(8,128)S(1)}, f32[128,1024]{1,0:T(8,128)S(1)},...) custom-call(bf16[2048,128]{1,0:T(8,128)(2,1)} %x_in.1, bf16[2048,128]{1,0:T(8,128)(2,1)} %dy_in.1, f32[1,128]{1,0:T(1,128)} %bitcast.2, ...), custom_call_target="tpu_custom_call" | custom-call | tf_op jit(solution)/shard_map/mlp_branch/pallas_call | solution.py:440
  70.5 1.7 %write_out.1 = (bf16[2048,128]{1,0:T(8,128)(2,1)}, bf16[2048,128]{1,0:T(8,128)(2,1)}, f32[128,1024]{1,0:T(8,128)}, f32[128,1024]{1,0:T(8,128)}, f32[1024,128]{1,0:T(8,128)}, /*index=5*/f32[1,128]{1,0:T(1,128)}) custom-call(bf16[2048,128]{1,0:T(8,128)(2,1)S(1)} %get-tuple-element.18.refs_0_, bf16[2048,128]{1,0:T(8,128)(2,1)S(1)} %get-tuple-element.19.refs_1_, ...), custom_call_target="tpu_custom_call" | custom-call | tf_op jit(solution)/shard_map/write_out/pallas_call | solution.py:467
